TPU v7x, 32 devices: a whole 2x2x4 slice. The times are simulated.
32 devices in a mesh: row: 8 (over z, x), col: 4 (over y, core).
Axes of the slice: x: 2, y: 2, z: 4, core: 2. Of those that a mesh axis runs over, the one named last changes fastest.
Arguments:
- tensor: float32 [32, 1024, 1024], P(None, 'row', 'col'), may hold values from -6 to 6
- initial_first: float32 [1024, 256], P('row'), may hold values from -6 to 6
- initial_second: float32 [1024, 256], P('col'), may hold values from -6 to 6
Outputs:
- factor_first: float32 [1024, 256], P('row')
- factor_second: float32 [1024, 256], P('col')
- factor_frames: float32 [32, 256], replicated
- weights: float32 [256], replicated
All inputs are finite; a program needn't handle non-finite values.
Results may differ from a plain program's by a relative error of at most 0.00024.
Values sent between devices are 32-bit elements; how exact they have to be, the bound alone decides.
A program may use at most 128 MiB of HBM per device.

v0:
```python
import functools
import math

import jax
import jax.numpy as jnp
from jax import lax
from jax.experimental import pallas as pl
from jax.experimental.pallas import tpu as pltpu
from jax.sharding import PartitionSpec as P

PASSES = 2
LANES = 128
PIVOTS = 16
MESH = pl.DeviceIdType.MESH
HIGHEST = lax.Precision.HIGHEST

epsilon = 1e-06


def product(a, b):
    return jnp.dot(a, b, precision=HIGHEST, preferred_element_type=jnp.float32)


def cross(a, b):
    return lax.dot_general(
        a, b, (((0,), (0,)), ((), ())), precision=HIGHEST, preferred_element_type=jnp.float32
    )


def invert(a, start, stop):
    size = a.shape[0]
    tiles = size // LANES
    row = lax.broadcasted_iota(jnp.int32, (PIVOTS, LANES), 0)
    lanes = [
        lax.broadcasted_iota(jnp.int32, (PIVOTS, LANES), 1) + q * LANES for q in range(tiles)
    ]
    wide = lax.broadcasted_iota(jnp.int32, (PIVOTS, size), 1)
    whole = lax.broadcasted_iota(jnp.int32, (size, size), 1)

    def step(g, carry):
        base = g * PIVOTS
        here = pl.ds(pl.multiple_of(base, PIVOTS), PIVOTS)
        rows = [a[here, q * LANES : (q + 1) * LANES] for q in range(tiles)]
        cols = []
        for t in range(PIVOTS):
            picked = sum(jnp.where(lanes[q] == base + t, rows[q], 0.0) for q in range(tiles))
            cols.append(
                jnp.broadcast_to(jnp.sum(picked, axis=1, keepdims=True), (PIVOTS, LANES))
            )
        work = []
        for q in range(tiles):
            place = lanes[q] - base
            inside = (place >= 0) & (place < PIVOTS)
            unit = jnp.where(place == row, 1.0, 0.0)
            work.append(jnp.where(inside, unit, rows[q]))
        for t in range(PIVOTS):
            pivot = 1.0 / jnp.broadcast_to(cols[t][t : t + 1, :], (PIVOTS, LANES))
            at = row == t

            def reduced(x):
                scaled = jnp.broadcast_to(x[t : t + 1, :], (PIVOTS, LANES)) * pivot
                return jnp.where(at, scaled, x - cols[t] * scaled)

            later = [reduced(cols[s]) for s in range(t + 1, PIVOTS)]
            work = [reduced(w) for w in work]
            cols[t + 1 :] = later
        solved = jnp.concatenate(work, axis=1)
        raw = a[here, :]
        inside = (wide >= base) & (wide < base + PIVOTS)
        left = jnp.where(inside, 0.0, jnp.where(wide < base, -raw, raw))
        kept = jnp.where((whole >= base) & (whole < base + PIVOTS), 0.0, a[...])
        a[...] = kept - cross(left, solved)
        a[here, :] = solved
        return carry

    lax.fori_loop(start, stop, step, 0)


def greet(sizes):
    barrier = pltpu.get_barrier_semaphore()
    for axis, n in sizes.items():
        me = lax.axis_index(axis)
        for d in range(1, n):
            pl.semaphore_signal(
                barrier, inc=1, device_id={axis: lax.rem(me + d, n)}, device_id_type=MESH
            )
    pl.semaphore_wait(barrier, sum(n - 1 for n in sizes.values()))


def scatter(axis, n, source, recv, sems):
    me = lax.axis_index(axis)
    chunk = recv.shape[1]
    copies = []
    for d in range(1, n):
        peer = lax.rem(me + d, n)
        copy = pltpu.make_async_remote_copy(
            src_ref=source.at[pl.ds(pl.multiple_of(peer * chunk, 8), chunk), :],
            dst_ref=recv.at[me],
            send_sem=sems.at[0, d - 1],
            recv_sem=sems.at[1, d - 1],
            device_id={axis: peer},
            device_id_type=MESH,
        )
        copy.start()
        copies.append(copy)
    recv[me] = source[pl.ds(pl.multiple_of(me * chunk, 8), chunk), :]
    return copies


def gather(axis, n, own, full, sems):
    me = lax.axis_index(axis)
    chunk = own.shape[0]
    place = pl.ds(pl.multiple_of(me * chunk, 8), chunk)
    full[place, :] = own
    copies = []
    for d in range(1, n):
        copy = pltpu.make_async_remote_copy(
            src_ref=full.at[place, :],
            dst_ref=full.at[place, :],
            send_sem=sems.at[0, d - 1],
            recv_sem=sems.at[1, d - 1],
            device_id={axis: lax.rem(me + d, n)},
            device_id_type=MESH,
        )
        copy.start()
        copies.append(copy)
    return copies


def finish(copies):
    for copy in copies:
        copy.wait()


def total(recv):
    result = recv[0]
    for s in range(1, recv.shape[0]):
        result = result + recv[s]
    return result


def total_blocks(full, n):
    chunk = full.shape[0] // n
    result = full[0:chunk, :]
    for s in range(1, n):
        result = result + full[s * chunk : (s + 1) * chunk, :]
    return result


def layout(sizes, frames, own_first, own_second, rank):
    row, col = sizes["row"], sizes["col"]
    square = (rank, rank)
    buffers = {
        "tens": (frames, own_first, own_second),
        "held": (frames, own_second, rank),
        "inv": square, "sums": (frames, rank),
        "gram_a": square, "recv_a": (row, rank // row, rank), "full_a": square,
        "gram_b": square, "recv_b": (col, rank // col, rank), "full_b": square,
        "terms_f": (own_first, rank), "recv_f": (col, own_first // col, rank),
        "raw_f": (own_first, rank), "parts_w": (row * 8, rank),
    }
    axes = {"a": row, "a2": row, "b": col, "b2": col, "f": col, "f2": col, "w": row}
    for p in range(PASSES):
        buffers.update({
            "parts_r%d" % p: (row * frames, rank), "parts_c%d" % p: (col * frames, rank),
            "terms_s%d" % p: (own_second, rank),
            "recv_s%d" % p: (row, own_second // row, rank), "raw_s%d" % p: (own_second, rank),
            "gram_g%d" % p: square, "recv_g%d" % p: (col, rank // col, rank),
            "full_g%d" % p: square,
        })
        axes.update({
            "r%d" % p: row, "c%d" % p: col, "s%d" % p: row, "t%d" % p: row,
            "g%d" % p: col, "h%d" % p: col,
        })
    names = list(buffers) + ["sem_" + name for name in axes] + ["sem_load"]
    shapes = [pltpu.VMEM(shape, jnp.float32) for shape in buffers.values()]
    shapes += [pltpu.SemaphoreType.DMA((2, n - 1)) for n in axes.values()]
    shapes += [pltpu.SemaphoreType.DMA((frames,))]
    return names, shapes


def kernel(sizes, names, tensor, first, second, first_out, second_out, frames_out, weights_out, *scratch):
    row, col = sizes["row"], sizes["col"]
    v = dict(zip(names, scratch))
    inv, sums, tens, held = v["inv"], v["sums"], v["tens"], v["held"]
    frames, own_first, own_second = tensor.shape
    rank = first.shape[1]
    rows_first, rows_second = own_first * row, own_second * col
    steps = rank // PIVOTS

    def load(k):
        return pltpu.make_async_copy(tensor.at[k], tens.at[k], v["sem_load"].at[k])

    def start_load(k, carry):
        load(k).start()
        return carry

    def contract(start, stop):
        group = math.gcd(stop - start, 4)

        def step(g, carry):
            ks = [start + g * group + u for u in range(group)]
            for k in ks:
                load(k).wait()
            parts = [cross(tens[k], first[...]) for k in ks]
            for k, part in zip(ks, parts):
                held[k] = part
                sums[pl.ds(k, 1), :] = jnp.sum(part * second[...], axis=0, keepdims=True)
            return carry

        lax.fori_loop(0, (stop - start) // group, step, 0)

    def frame_terms(raw):
        def step(k, carry):
            sums[pl.ds(k, 1), :] = jnp.sum(held[k] * raw[...], axis=0, keepdims=True)
            return carry

        lax.fori_loop(0, frames, step, 0)

    def second_terms(out):
        block = math.gcd(own_second, 64)
        for c in range(0, own_second, block):
            def step(k, total):
                return total + held[k, c : c + block, :] * frames_out[pl.ds(k, 1), :]

            out[c : c + block, :] = lax.fori_loop(
                0, frames, step, jnp.zeros((block, rank), jnp.float32), unroll=4
            )

    def first_terms(raw, start, stop):
        group = math.gcd(stop - start, 4)

        def step(g, carry):
            base = start + g * group
            stacked = tens[pl.ds(base, group)].reshape(group * own_first, own_second)
            part = product(stacked, raw[...])
            v["terms_f"][...] += sum(
                part[u * own_first : (u + 1) * own_first, :] * frames_out[pl.ds(base + u, 1), :]
                for u in range(group)
            )
            return carry

        lax.fori_loop(0, (stop - start) // group, step, 0)

    def solve_frames(frame_sums):
        raw = product(frame_sums, inv[...]) * (1.0 / math.sqrt(rows_first * rows_second))
        normed = raw / jnp.sqrt(jnp.mean(raw * raw, axis=0, keepdims=True) + epsilon)
        frames_out[...] = normed
        return cross(normed, normed) / frames

    lax.fori_loop(0, frames, start_load, 0)
    v["gram_a"][...] = cross(first[...], first[...])
    v["gram_b"][...] = cross(second[...], second[...])
    greet(sizes)
    go_a = scatter("row", row, v["gram_a"], v["recv_a"], v["sem_a"])
    go_b = scatter("col", col, v["gram_b"], v["recv_b"], v["sem_b"])
    contract(0, frames // 2)
    finish(go_a)
    go_a = gather("row", row, total(v["recv_a"]), v["full_a"], v["sem_a2"])
    finish(go_b)
    go_b = gather("col", col, total(v["recv_b"]), v["full_b"], v["sem_b2"])
    contract(frames // 2, frames)
    finish(go_a)
    finish(go_b)
    first_gram = v["gram_a"]
    first_gram[...] = v["full_a"][...] * (1.0 / rows_first)
    second_gram = v["full_b"][...] * (1.0 / rows_second)
    wide = None
    for p in range(PASSES):
        here = str(p)
        if p == 0:
            go_r = gather("row", row, sums[...], v["parts_r0"], v["sem_r0"])
            inv[...] = first_gram[...] * second_gram
            invert(inv, 0, steps // 2)
            finish(go_r)
            go_c = gather(
                "col", col, total_blocks(v["parts_r0"], row), v["parts_c0"], v["sem_c0"]
            )
            invert(inv, steps // 2, steps)
        else:
            inv[...] = first_gram[...] * second_gram
            invert(inv, 0, steps)
        finish(go_c)
        frame_sums = total_blocks(v["parts_c" + here], col)
        if wide is not None:
            frame_sums = frame_sums / wide
        frame_gram = solve_frames(frame_sums)
        second_terms(v["terms_s" + here])
        go_s = scatter(
            "row", row, v["terms_s" + here], v["recv_s" + here], v["sem_s" + here]
        )
        inv[...] = first_gram[...] * frame_gram
        invert(inv, 0, steps)
        finish(go_s)
        solved = product(total(v["recv_s" + here]), inv[...])
        raw = v["raw_s" + here]
        go_s = gather(
            "row", row, solved * (1.0 / math.sqrt(rows_first * frames)), raw, v["sem_t" + here]
        )
        finish(go_s)
        v["gram_g" + here][...] = cross(raw[...], raw[...])
        go_g = scatter(
            "col", col, v["gram_g" + here], v["recv_g" + here], v["sem_g" + here]
        )
        last = p + 1 == PASSES
        if last:
            v["terms_f"][...] = jnp.zeros((own_first, rank), jnp.float32)
            first_terms(raw, 0, frames // 2)
        else:
            later = str(p + 1)
            frame_terms(raw)
            go_r = gather("row", row, sums[...], v["parts_r" + later], v["sem_r" + later])
        finish(go_g)
        go_g = gather(
            "col", col, total(v["recv_g" + here]), v["full_g" + here], v["sem_h" + here]
        )
        if last:
            first_terms(raw, frames // 2, frames)
            go_f = scatter("col", col, v["terms_f"], v["recv_f"], v["sem_f"])
        else:
            finish(go_r)
            go_c = gather(
                "col", col, total_blocks(v["parts_r" + later], row),
                v["parts_c" + later], v["sem_c" + later],
            )
        finish(go_g)
        gram = v["full_g" + here][...] * (1.0 / rows_second)
        down = lax.broadcasted_iota(jnp.int32, (rank, rank), 0)
        across = lax.broadcasted_iota(jnp.int32, (rank, rank), 1)
        diagonal = jnp.where(down == across, gram, 0.0)
        wide = jnp.sqrt(jnp.sum(diagonal, axis=0, keepdims=True) + epsilon)
        tall = jnp.sqrt(jnp.sum(diagonal, axis=1, keepdims=True) + epsilon)
        second_gram = gram / wide / tall
    inv[...] = second_gram * frame_gram
    second_out[...] = raw[...] / wide
    invert(inv, 0, steps)
    finish(go_f)
    solved = product(total(v["recv_f"]) / wide, inv[...])
    go_f = gather(
        "col", col, solved * (1.0 / math.sqrt(rows_second * frames)), v["raw_f"], v["sem_f2"]
    )
    finish(go_f)
    raw = v["raw_f"][...]
    squares = jnp.sum(raw * raw, axis=0, keepdims=True)
    go_w = gather("row", row, jnp.broadcast_to(squares, (8, rank)), v["parts_w"], v["sem_w"])
    finish(go_w)
    weights = jnp.sqrt(total_blocks(v["parts_w"], row) * (1.0 / rows_first) + epsilon)
    weights_out[...] = weights
    first_out[...] = raw / weights[0:1, :]


def body(sizes, tensor, initial_first, initial_second):
    frames, own_first, own_second = tensor.shape
    rank = initial_first.shape[1]
    names, scratch = layout(sizes, frames, own_first, own_second, rank)
    vmem = pl.BlockSpec(memory_space=pltpu.VMEM)
    outs = ((own_first, rank), (own_second, rank), (frames, rank), (8, rank))
    factor_first, second, factor_frames, weights = pl.pallas_call(
        functools.partial(kernel, sizes, names),
        out_shape=[jax.ShapeDtypeStruct(shape, jnp.float32) for shape in outs],
        in_specs=[pl.BlockSpec(memory_space=pl.ANY), vmem, vmem],
        out_specs=[vmem] * len(outs),
        scratch_shapes=scratch,
        compiler_params=pltpu.CompilerParams(
            collective_id=0, has_side_effects=True, vmem_limit_bytes=48 * 1024 * 1024
        ),
        name="als",
    )(tensor, initial_first, initial_second)
    return (factor_first, second, factor_frames, weights[0])


def solution(mesh):
    sizes = {"row": mesh.shape["row"], "col": mesh.shape["col"]}
    placed = (P(None, "row", "col"), P("row", None), P("col", None))
    return jax.shard_map(
        functools.partial(body, sizes),
        mesh=mesh,
        in_specs=placed,
        out_specs=(P("row", None), P("col", None), P(), P()),
        check_vma=False,
    )
```

profile of v0, /device:TPU:0, one launch (start us, length us, event | category | flops | bytes accessed | tf_op | source)
XLA Modules:
  0.0 130.8 jit_solution(10077121806767231288)
XLA Ops:
  0.6 0.0 copy-start
  0.6 2.2 %copy-done = f32[32,128,256]{2,1,0:T(8,128)S(1)} copy-done((f32[32,128,256]{2,1,0:T(8,128)S(1)}, f32[32,128,256]{2,1,0:T(8,128)}, u32[]{:S(2)}) %copy-start) | copy-done | bytes 4194328
  2.8 0.0 copy-start.1
  2.8 0.9 copy-done.1
  3.8 0.0 copy-start.2
  3.8 0.9 copy-done.2
  4.7 123.5 %als.1 = (f32[128,256]{1,0:T(8,128)S(1)}, f32[256,256]{1,0:T(8,128)S(1)}, f32[32,256]{1,0:T(8,128)S(1)}, f32[8,256]{1,0:T(8,128)S(1)}) custom-call(f32[32,128,256]{2,1,0:T(8,128)S(1)} %copy-done, f32[128,256]{1,0:T(8,128)S(1)} %copy-done.2, f32[256,256]{1,0:T(8,128)S(1)} %copy-done.1), custom_call_target="tpu_custom_call" | custom-call | tf_op jit(solution)/shard_map/als/pallas_call | solution.py:358
  128.2 0.6 slice.3
  128.8 0.7 copy.10
  129.4 0.7 copy.11
  130.1 0.6 copy.12
Async XLA Ops:
  0.6 2.2 %copy-start = (f32[32,128,256]{2,1,0:T(8,128)S(1)}, f32[32,128,256]{2,1,0:T(8,128)}, u32[]{:S(2)}) copy-start(f32[32,128,256]{2,1,0:T(8,128)} %tensor.1) | copy-start | bytes 12582916
  2.8 0.9 copy-start.1
  3.8 0.9 copy-start.2
where the time goes:
time: 131 us
  Pallas kernels  124 us (95%)
  local copies, waits for them, and re-layouts  6.57 us (5%)
    pallas_call x1, Pallas kernels, body(): pl.pallas_call(functools.partial(kernel, sizes, names), out_shape=[jax.Sh...  124 us
    unnamed x9, local copies, waits for them, and re-layouts  6.01 us

commit v1 on v0

v1 whole, which is shorter than its diff:
```python
import functools
import math

import jax
import jax.numpy as jnp
from jax import lax
from jax.experimental import pallas as pl
from jax.experimental.pallas import tpu as pltpu
from jax.sharding import PartitionSpec as P

PASSES = 2
LANES = 128
PIVOTS = 16
MESH = pl.DeviceIdType.MESH
HIGHEST = lax.Precision.HIGHEST
HIGH = lax.Precision.HIGH

epsilon = 1e-06


def product(a, b, precision=HIGHEST):
    return jnp.dot(a, b, precision=precision, preferred_element_type=jnp.float32)


def cross(a, b, precision=HIGHEST):
    return lax.dot_general(
        a, b, (((0,), (0,)), ((), ())), precision=precision, preferred_element_type=jnp.float32
    )


def split(x):
    high = x.astype(jnp.bfloat16)
    rest = x - high.astype(jnp.float32)
    mid = rest.astype(jnp.bfloat16)
    return high, mid, (rest - mid.astype(jnp.float32)).astype(jnp.bfloat16)


def outer(left, right):
    h, m, l = split(left)
    hh, mm, ll = split(right)
    return lax.dot_general(
        jnp.concatenate([h, h, m, h, m, l], axis=0),
        jnp.concatenate([hh, mm, hh, ll, mm, hh], axis=0),
        (((0,), (0,)), ((), ())), preferred_element_type=jnp.float32,
    )


def invert(a, start, stop):
    size = a.shape[0]
    tiles = size // LANES
    row = lax.broadcasted_iota(jnp.int32, (PIVOTS, LANES), 0)
    lanes = [
        lax.broadcasted_iota(jnp.int32, (PIVOTS, LANES), 1) + q * LANES for q in range(tiles)
    ]
    wide = lax.broadcasted_iota(jnp.int32, (PIVOTS, size), 1)
    whole = lax.broadcasted_iota(jnp.int32, (size, size), 1)

    def step(g, carry):
        base = g * PIVOTS
        here = pl.ds(pl.multiple_of(base, PIVOTS), PIVOTS)
        rows = [a[here, q * LANES : (q + 1) * LANES] for q in range(tiles)]
        cols = []
        for t in range(PIVOTS):
            picked = sum(jnp.where(lanes[q] == base + t, rows[q], 0.0) for q in range(tiles))
            cols.append(
                jnp.broadcast_to(jnp.sum(picked, axis=1, keepdims=True), (PIVOTS, LANES))
            )
        work = []
        for q in range(tiles):
            place = lanes[q] - base
            inside = (place >= 0) & (place < PIVOTS)
            unit = jnp.where(place == row, 1.0, 0.0)
            work.append(jnp.where(inside, unit, rows[q]))
        for t in range(PIVOTS):
            pivot = 1.0 / jnp.broadcast_to(cols[t][t : t + 1, :], (PIVOTS, LANES))
            at = row == t

            def reduced(x):
                scaled = jnp.broadcast_to(x[t : t + 1, :], (PIVOTS, LANES)) * pivot
                return jnp.where(at, scaled, x - cols[t] * scaled)

            later = [reduced(cols[s]) for s in range(t + 1, PIVOTS)]
            work = [reduced(w) for w in work]
            cols[t + 1 :] = later
        solved = jnp.concatenate(work, axis=1)
        raw = a[here, :]
        inside = (wide >= base) & (wide < base + PIVOTS)
        left = jnp.where(inside, 0.0, jnp.where(wide < base, -raw, raw))
        kept = jnp.where((whole >= base) & (whole < base + PIVOTS), 0.0, a[...])
        a[...] = kept - outer(left, solved)
        a[here, :] = solved
        return carry

    lax.fori_loop(start, stop, step, 0)


def greet(sizes):
    barrier = pltpu.get_barrier_semaphore()
    for axis, n in sizes.items():
        me = lax.axis_index(axis)
        for d in range(1, n):
            pl.semaphore_signal(
                barrier, inc=1, device_id={axis: lax.rem(me + d, n)}, device_id_type=MESH
            )


def greeted(sizes):
    pl.semaphore_wait(pltpu.get_barrier_semaphore(), sum(n - 1 for n in sizes.values()))


def send(source, target, sems, at, device):
    copy = pltpu.make_async_remote_copy(
        src_ref=source, dst_ref=target, send_sem=sems.at[0, at], recv_sem=sems.at[1, at],
        device_id=device, device_id_type=MESH,
    )
    copy.start()
    return copy


def span(index, chunk):
    return pl.ds(pl.multiple_of(index * chunk, 8), chunk)


def scatter(axis, n, source, recv, sems, offset=0):
    me = lax.axis_index(axis)
    chunk = recv.shape[1]
    copies = []
    for d in range(1, n):
        peer = lax.rem(me + d, n)
        there = pl.ds(pl.multiple_of(offset + peer * chunk, 8), chunk)
        copies.append(send(source.at[there, :], recv.at[me], sems, d - 1, {axis: peer}))
    recv[me] = source[pl.ds(pl.multiple_of(offset + me * chunk, 8), chunk), :]
    return copies


def gather(axis, n, own, full, sems, offset=0):
    me = lax.axis_index(axis)
    chunk = own.shape[0]
    place = pl.ds(pl.multiple_of(offset + me * chunk, 8), chunk)
    full[place, :] = own
    return [
        send(full.at[place, :], full.at[place, :], sems, d - 1, {axis: lax.rem(me + d, n)})
        for d in range(1, n)
    ]


def finish(copies):
    for copy in copies:
        copy.wait()


def total(recv):
    result = recv[0]
    for s in range(1, recv.shape[0]):
        result = result + recv[s]
    return result


def total_blocks(full, n):
    chunk = full.shape[0] // n
    result = full[0:chunk, :]
    for s in range(1, n):
        result = result + full[s * chunk : (s + 1) * chunk, :]
    return result


class Twin:
    def __init__(self, col):
        self.count = col // 2
        me = lax.axis_index("col")
        self.core = lax.rem(me, 2)
        self.chip = me // 2
        self.partner = {"col": self.chip * 2 + 1 - self.core}
        self.others = [
            {"col": lax.rem(self.chip + d, self.count) * 2 + self.core}
            for d in range(1, self.count)
        ]


def halves_out(twin, gram, recv, sems):
    half = gram.shape[0] // 2
    return [send(gram.at[span(1 - twin.core, half), :], recv, sems, 0, twin.partner)]


def halves_across(twin, gram, recv, across, sems):
    half = gram.shape[0] // 2
    across[twin.chip] = gram[span(twin.core, half), :] + recv[...]
    here = across.at[twin.chip]
    return [send(here, here, sems, d, peer) for d, peer in enumerate(twin.others)]


def halves_back(twin, full, sems):
    half = full.shape[0] // 2
    mine = full.at[span(twin.core, half), :]
    return [send(mine, mine, sems, 0, twin.partner)]


def layout(sizes, frames, own_first, own_second, rank):
    row, col = sizes["row"], sizes["col"]
    square = (rank, rank)
    half = rank // 2
    chips = col // 2
    buffers = {
        "tens": (frames, own_first, own_second),
        "held": (frames, own_second, rank),
        "inv": square, "sums": (frames, rank),
        "gram_a": square, "recv_a": (row, half // row, rank), "full_a": square,
        "gram_b": square, "recv_b": (half, rank), "across_b": (chips, half, rank),
        "full_b": square,
        "terms_f": (own_first, rank), "recv_f": (col, own_first // col, rank),
        "full_f": (own_first, rank), "parts_w": (row * 8, rank),
    }
    axes = {
        "a": row, "a2": row, "a3": 2, "b": 2, "b2": chips, "b3": 2, "f": col, "f2": col,
        "w": row,
    }
    for p in range(PASSES):
        buffers.update({
            "parts_r%d" % p: (row * frames, rank), "parts_c%d" % p: (col * frames, rank),
            "raw_s%d" % p: (own_second, rank),
            "gram_g%d" % p: square, "recv_g%d" % p: (half, rank),
            "across_g%d" % p: (chips, half, rank), "full_g%d" % p: square,
        })
        axes.update({
            "r%d" % p: row, "c%d" % p: col, "g%d" % p: 2, "h%d" % p: chips, "i%d" % p: 2,
        })
        for q in range(rank // LANES):
            buffers.update({
                "terms_s%d%d" % (p, q): (own_second, LANES),
                "recv_s%d%d" % (p, q): (row, own_second // row, LANES),
                "full_s%d%d" % (p, q): (own_second, LANES),
            })
            axes.update({"s%d%d" % (p, q): row, "t%d%d" % (p, q): row})
    names = list(buffers) + ["sem_" + name for name in axes] + ["sem_load"]
    shapes = [pltpu.VMEM(shape, jnp.float32) for shape in buffers.values()]
    shapes += [pltpu.SemaphoreType.DMA((2, max(n - 1, 1))) for n in axes.values()]
    shapes += [pltpu.SemaphoreType.DMA((frames,))]
    return names, shapes


def kernel(sizes, names, tensor, first, second, first_out, second_out, frames_out, weights_out, *scratch):
    row, col = sizes["row"], sizes["col"]
    v = dict(zip(names, scratch))
    inv, sums, tens, held = v["inv"], v["sums"], v["tens"], v["held"]
    frames, own_first, own_second = tensor.shape
    rank = first.shape[1]
    half = rank // 2
    tiles = rank // LANES
    rows_first, rows_second = own_first * row, own_second * col
    steps = rank // PIVOTS
    twin = Twin(col)

    def load(k):
        return pltpu.make_async_copy(tensor.at[k], tens.at[k], v["sem_load"].at[k])

    def start_load(k, carry):
        load(k).start()
        return carry

    def contract(start, stop):
        group = math.gcd(stop - start, 4)

        def step(g, carry):
            ks = [start + g * group + u for u in range(group)]
            for k in ks:
                load(k).wait()
            parts = [cross(tens[k], first[...], HIGH) for k in ks]
            for k, part in zip(ks, parts):
                held[k] = part
                sums[pl.ds(k, 1), :] = jnp.sum(part * second[...], axis=0, keepdims=True)
            return carry

        lax.fori_loop(0, (stop - start) // group, step, 0)

    def frame_terms(raw, start, stop):
        def step(k, carry):
            sums[pl.ds(k, 1), :] = jnp.sum(held[k] * raw[...], axis=0, keepdims=True)
            return carry

        lax.fori_loop(start, stop, step, 0, unroll=4)

    def second_terms(out, q):
        block = math.gcd(own_second, 128)
        here = slice(q * LANES, (q + 1) * LANES)
        for c in range(0, own_second, block):
            def step(k, total):
                return total + held[k, c : c + block, here] * frames_out[pl.ds(k, 1), :][:, here]

            out[c : c + block, :] = lax.fori_loop(
                0, frames, step, jnp.zeros((block, LANES), jnp.float32), unroll=4
            )

    def first_terms(raw, start, stop):
        group = math.gcd(stop - start, 4)

        def step(g, carry):
            base = start + g * group
            stacked = tens[pl.ds(base, group)].reshape(group * own_first, own_second)
            part = product(stacked, raw[...], HIGH)
            v["terms_f"][...] += sum(
                part[u * own_first : (u + 1) * own_first, :] * frames_out[pl.ds(base + u, 1), :]
                for u in range(group)
            )
            return carry

        lax.fori_loop(0, (stop - start) // group, step, 0)

    def solve_frames(frame_sums):
        raw = product(frame_sums, inv[...]) * (1.0 / math.sqrt(rows_first * rows_second))
        normed = raw / jnp.sqrt(jnp.mean(raw * raw, axis=0, keepdims=True) + epsilon)
        frames_out[...] = normed
        return cross(normed, normed) / frames

    greet(sizes)
    lax.fori_loop(0, frames, start_load, 0)
    v["gram_a"][...] = cross(first[...], first[...])
    v["gram_b"][...] = cross(second[...], second[...])
    contract(0, frames // 4)
    greeted(sizes)
    offset = twin.core * half
    go_a = scatter("row", row, v["gram_a"], v["recv_a"], v["sem_a"], offset)
    go_b = halves_out(twin, v["gram_b"], v["recv_b"], v["sem_b"])
    contract(frames // 4, frames * 5 // 8)
    finish(go_b)
    go_b = halves_across(twin, v["gram_b"], v["recv_b"], v["across_b"], v["sem_b2"])
    finish(go_a)
    go_a = gather("row", row, total(v["recv_a"]), v["full_a"], v["sem_a2"], offset)
    contract(frames * 5 // 8, frames)
    go_r = gather("row", row, sums[...], v["parts_r0"], v["sem_r0"])
    finish(go_b)
    v["full_b"][span(twin.core, half), :] = total(v["across_b"])
    go_b = halves_back(twin, v["full_b"], v["sem_b3"])
    finish(go_a)
    go_a = halves_back(twin, v["full_a"], v["sem_a3"])
    finish(go_b)
    finish(go_a)
    first_gram = v["gram_a"]
    first_gram[...] = v["full_a"][...] * (1.0 / rows_first)
    second_gram = v["full_b"][...] * (1.0 / rows_second)
    wide = None
    for p in range(PASSES):
        here = str(p)
        split_at = steps // 8 if p == 0 else steps // 2
        inv[...] = first_gram[...] * second_gram
        invert(inv, 0, split_at)
        finish(go_r)
        go_c = gather(
            "col", col, total_blocks(v["parts_r" + here], row), v["parts_c" + here],
            v["sem_c" + here],
        )
        invert(inv, split_at, steps)
        finish(go_c)
        frame_sums = total_blocks(v["parts_c" + here], col)
        if wide is not None:
            frame_sums = frame_sums / wide
        frame_gram = solve_frames(frame_sums)
        parts = [here + str(q) for q in range(tiles)]
        go_s = []
        for q, part in enumerate(parts):
            second_terms(v["terms_s" + part], q)
            go_s.append(scatter(
                "row", row, v["terms_s" + part], v["recv_s" + part], v["sem_s" + part]
            ))
        inv[...] = first_gram[...] * frame_gram
        go_t = []
        at = 0
        for q, part in enumerate(parts):
            invert(inv, at, steps * (5 + 2 * q) // 8)
            at = steps * (5 + 2 * q) // 8
            finish(go_s[q])
            go_t.append(gather(
                "row", row, total(v["recv_s" + part]), v["full_s" + part], v["sem_t" + part]
            ))
        invert(inv, at, steps)
        for copies in go_t:
            finish(copies)
        raw = v["raw_s" + here]
        summed = jnp.concatenate([v["full_s" + part][...] for part in parts], axis=1)
        raw[...] = product(summed, inv[...]) * (1.0 / math.sqrt(rows_first * frames))
        gram_g, recv_g, across_g, full_g = (
            v[name + here] for name in ("gram_g", "recv_g", "across_g", "full_g")
        )
        gram_g[...] = cross(raw[...], raw[...])
        go_g = halves_out(twin, gram_g, recv_g, v["sem_g" + here])
        last = p + 1 == PASSES
        if last:
            v["terms_f"][...] = jnp.zeros((own_first, rank), jnp.float32)
            first_terms(raw, 0, frames // 4)
        else:
            later = str(p + 1)
            frame_terms(raw, 0, frames // 2)
        finish(go_g)
        go_g = halves_across(twin, gram_g, recv_g, across_g, v["sem_h" + here])
        if last:
            first_terms(raw, frames // 4, frames)
            go_f = scatter("col", col, v["terms_f"], v["recv_f"], v["sem_f"])
        else:
            frame_terms(raw, frames // 2, frames)
            go_r = gather("row", row, sums[...], v["parts_r" + later], v["sem_r" + later])
        finish(go_g)
        full_g[span(twin.core, half), :] = total(across_g)
        go_g = halves_back(twin, full_g, v["sem_i" + here])
        finish(go_g)
        gram = full_g[...] * (1.0 / rows_second)
        down = lax.broadcasted_iota(jnp.int32, (rank, rank), 0)
        across = lax.broadcasted_iota(jnp.int32, (rank, rank), 1)
        diagonal = jnp.where(down == across, gram, 0.0)
        wide = jnp.sqrt(jnp.sum(diagonal, axis=0, keepdims=True) + epsilon)
        tall = jnp.sqrt(jnp.sum(diagonal, axis=1, keepdims=True) + epsilon)
        second_gram = gram / wide / tall
    inv[...] = second_gram * frame_gram
    second_out[...] = raw[...] / wide
    invert(inv, 0, steps // 4)
    finish(go_f)
    go_f = gather("col", col, total(v["recv_f"]), v["full_f"], v["sem_f2"])
    invert(inv, steps // 4, steps)
    finish(go_f)
    raw = product(v["full_f"][...] / wide, inv[...]) * (1.0 / math.sqrt(rows_second * frames))
    squares = jnp.sum(raw * raw, axis=0, keepdims=True)
    go_w = gather("row", row, jnp.broadcast_to(squares, (8, rank)), v["parts_w"], v["sem_w"])
    first_out[...] = raw
    finish(go_w)
    weights = jnp.sqrt(total_blocks(v["parts_w"], row) * (1.0 / rows_first) + epsilon)
    weights_out[...] = weights
    first_out[...] = first_out[...] / weights[0:1, :]


def body(sizes, tensor, initial_first, initial_second):
    frames, own_first, own_second = tensor.shape
    rank = initial_first.shape[1]
    names, scratch = layout(sizes, frames, own_first, own_second, rank)
    vmem = pl.BlockSpec(memory_space=pltpu.VMEM)
    outs = ((own_first, rank), (own_second, rank), (frames, rank), (8, rank))
    factor_first, second, factor_frames, weights = pl.pallas_call(
        functools.partial(kernel, sizes, names),
        out_shape=[jax.ShapeDtypeStruct(shape, jnp.float32) for shape in outs],
        in_specs=[pl.BlockSpec(memory_space=pl.ANY), vmem, vmem],
        out_specs=[vmem] * len(outs),
        scratch_shapes=scratch,
        compiler_params=pltpu.CompilerParams(
            collective_id=0, has_side_effects=True, vmem_limit_bytes=48 * 1024 * 1024
        ),
        name="als",
    )(tensor, initial_first, initial_second)
    return (factor_first, second, factor_frames, weights[0])


def solution(mesh):
    sizes = {"row": mesh.shape["row"], "col": mesh.shape["col"]}
    placed = (P(None, "row", "col"), P("row", None), P("col", None))
    return jax.shard_map(
        functools.partial(body, sizes),
        mesh=mesh,
        in_specs=placed,
        out_specs=(P("row", None), P("col", None), P(), P()),
        check_vma=False,
    )
```

time: 131 us -> 106 us (0.81)
  Pallas kernels: 124 us -> 98.3 us
    pallas_call x1, Pallas kernels: 124 us -> 98.3 us  [body(): pl.pallas_call(functools.partial(kernel, sizes, names), out_shape=[jax.Sh...]
where the time goes in v1:
time: 106 us
  Pallas kernels  98.3 us (93%)
  local copies, waits for them, and re-layouts  6.57 us (6%)
    pallas_call x1, Pallas kernels, body(): pl.pallas_call(functools.partial(kernel, sizes, names), out_shape=[jax.Sh...  98.3 us
    unnamed x9, local copies, waits for them, and re-layouts  6.01 us

profile of v1, /device:TPU:0, one launch (start us, length us, event | category | flops | bytes accessed | tf_op | source)
XLA Modules:
  0.0 105.5 jit_solution(4356656298483744129)
XLA Ops:
  0.6 0.0 copy-start
  0.6 2.2 %copy-done = f32[32,128,256]{2,1,0:T(8,128)S(1)} copy-done((f32[32,128,256]{2,1,0:T(8,128)S(1)}, f32[32,128,256]{2,1,0:T(8,128)}, u32[]{:S(2)}) %copy-start) | copy-done | bytes 4194328
  2.8 0.0 copy-start.1
  2.8 0.9 copy-done.1
  3.8 0.0 copy-start.2
  3.8 0.9 copy-done.2
  4.7 98.3 %als.1 = (f32[128,256]{1,0:T(8,128)S(1)}, f32[256,256]{1,0:T(8,128)S(1)}, f32[32,256]{1,0:T(8,128)S(1)}, f32[8,256]{1,0:T(8,128)S(1)}) custom-call(f32[32,128,256]{2,1,0:T(8,128)S(1)} %copy-done, f32[128,256]{1,0:T(8,128)S(1)} %copy-done.2, f32[256,256]{1,0:T(8,128)S(1)} %copy-done.1), custom_call_target="tpu_custom_call" | custom-call | tf_op jit(solution)/shard_map/als/pallas_call | solution.py:434
  103.0 0.6 slice.3
  103.6 0.7 copy.10
  104.2 0.7 copy.11
  104.9 0.6 copy.12
Async XLA Ops:
  0.6 2.2 %copy-start = (f32[32,128,256]{2,1,0:T(8,128)S(1)}, f32[32,128,256]{2,1,0:T(8,128)}, u32[]{:S(2)}) copy-start(f32[32,128,256]{2,1,0:T(8,128)} %tensor.1) | copy-start | bytes 12582916
  2.8 0.9 copy-start.1
  3.8 0.9 copy-start.2

commit v2 on v1

--- a/solution.py
+++ b/solution.py
@@ -11,6 +11,7 @@
 PASSES = 2
 LANES = 128
 PIVOTS = 16
+GROUP = 4
 MESH = pl.DeviceIdType.MESH
 HIGHEST = lax.Precision.HIGHEST
 HIGH = lax.Precision.HIGH
@@ -144,6 +145,13 @@
     ]
 
 
+def spread(axis, n, line, parts, sems):
+    me = lax.axis_index(axis)
+    here = parts.at[me, pl.ds(0, 1), :]
+    parts[me, 0:1, :] = line
+    return [send(here, here, sems, d - 1, {axis: lax.rem(me + d, n)}) for d in range(1, n)]
+
+
 def finish(copies):
     for copy in copies:
         copy.wait()
@@ -203,12 +211,15 @@
     buffers = {
         "tens": (frames, own_first, own_second),
         "held": (frames, own_second, rank),
+        "first": (own_first, rank), "second": (own_second, rank),
+        "first_out": (own_first, rank), "second_out": (own_second, rank),
+        "frames_out": (frames, rank), "weights_out": (8, rank),
         "inv": square, "sums": (frames, rank),
         "gram_a": square, "recv_a": (row, half // row, rank), "full_a": square,
         "gram_b": square, "recv_b": (half, rank), "across_b": (chips, half, rank),
         "full_b": square,
         "terms_f": (own_first, rank), "recv_f": (col, own_first // col, rank),
-        "full_f": (own_first, rank), "parts_w": (row * 8, rank),
+        "full_f": (own_first, rank), "parts_w": (row, 8, rank),
     }
     axes = {
         "a": row, "a2": row, "a3": 2, "b": 2, "b2": chips, "b3": 2, "f": col, "f2": col,
@@ -231,17 +242,20 @@
                 "full_s%d%d" % (p, q): (own_second, LANES),
             })
             axes.update({"s%d%d" % (p, q): row, "t%d%d" % (p, q): row})
-    names = list(buffers) + ["sem_" + name for name in axes] + ["sem_load"]
+    names = list(buffers) + ["sem_" + name for name in axes] + ["sem_load", "sem_move"]
     shapes = [pltpu.VMEM(shape, jnp.float32) for shape in buffers.values()]
     shapes += [pltpu.SemaphoreType.DMA((2, max(n - 1, 1))) for n in axes.values()]
-    shapes += [pltpu.SemaphoreType.DMA((frames,))]
+    shapes += [pltpu.SemaphoreType.DMA((frames // math.gcd(frames, GROUP),))]
+    shapes += [pltpu.SemaphoreType.DMA((6,))]
     return names, shapes
 
 
-def kernel(sizes, names, tensor, first, second, first_out, second_out, frames_out, weights_out, *scratch):
+def kernel(sizes, names, tensor, first_in, second_in, first_to, second_to, frames_to, weights_to, *scratch):
     row, col = sizes["row"], sizes["col"]
     v = dict(zip(names, scratch))
     inv, sums, tens, held = v["inv"], v["sums"], v["tens"], v["held"]
+    first, second, frames_out, weights_out = v["first"], v["second"], v["frames_out"], v["weights_out"]
+    first_out, second_out = v["first_out"], v["second_out"]
     frames, own_first, own_second = tensor.shape
     rank = first.shape[1]
     half = rank // 2
@@ -250,27 +264,29 @@
     steps = rank // PIVOTS
     twin = Twin(col)
 
-    def load(k):
-        return pltpu.make_async_copy(tensor.at[k], tens.at[k], v["sem_load"].at[k])
-
-    def start_load(k, carry):
-        load(k).start()
-        return carry
+    group = math.gcd(frames, GROUP)
+    loads = frames // group
+
+    def load(g):
+        block = pl.ds(g * group, group)
+        return pltpu.make_async_copy(tensor.at[block], tens.at[block], v["sem_load"].at[g])
+
+    def move(source, target, at):
+        copy = pltpu.make_async_copy(source, target, v["sem_move"].at[at])
+        copy.start()
+        return copy
 
     def contract(start, stop):
-        group = math.gcd(stop - start, 4)
-
         def step(g, carry):
-            ks = [start + g * group + u for u in range(group)]
-            for k in ks:
-                load(k).wait()
+            load(g).wait()
+            ks = [g * group + u for u in range(group)]
             parts = [cross(tens[k], first[...], HIGH) for k in ks]
             for k, part in zip(ks, parts):
                 held[k] = part
                 sums[pl.ds(k, 1), :] = jnp.sum(part * second[...], axis=0, keepdims=True)
             return carry
 
-        lax.fori_loop(0, (stop - start) // group, step, 0)
+        lax.fori_loop(start, stop, step, 0)
 
     def frame_terms(raw, start, stop):
         def step(k, carry):
@@ -312,20 +328,24 @@
         return cross(normed, normed) / frames
 
     greet(sizes)
-    lax.fori_loop(0, frames, start_load, 0)
-    v["gram_a"][...] = cross(first[...], first[...])
-    v["gram_b"][...] = cross(second[...], second[...])
-    contract(0, frames // 4)
+    come = [move(first_in, first, 0), move(second_in, second, 1)]
+    for g in range(loads):
+        load(g).start()
+    come[0].wait()
+    v["gram_a"][...] = cross(first[...], first[...], HIGH)
+    come[1].wait()
+    v["gram_b"][...] = cross(second[...], second[...], HIGH)
+    contract(0, loads // 4)
     greeted(sizes)
     offset = twin.core * half
     go_a = scatter("row", row, v["gram_a"], v["recv_a"], v["sem_a"], offset)
     go_b = halves_out(twin, v["gram_b"], v["recv_b"], v["sem_b"])
-    contract(frames // 4, frames * 5 // 8)
+    contract(loads // 4, loads * 5 // 8)
     finish(go_b)
     go_b = halves_across(twin, v["gram_b"], v["recv_b"], v["across_b"], v["sem_b2"])
     finish(go_a)
     go_a = gather("row", row, total(v["recv_a"]), v["full_a"], v["sem_a2"], offset)
-    contract(frames * 5 // 8, frames)
+    contract(loads * 5 // 8, loads)
     go_r = gather("row", row, sums[...], v["parts_r0"], v["sem_r0"])
     finish(go_b)
     v["full_b"][span(twin.core, half), :] = total(v["across_b"])
@@ -340,7 +360,7 @@
     wide = None
     for p in range(PASSES):
         here = str(p)
-        split_at = steps // 8 if p == 0 else steps // 2
+        split_at = 0 if p == 0 else steps // 2
         inv[...] = first_gram[...] * second_gram
         invert(inv, 0, split_at)
         finish(go_r)
@@ -376,11 +396,11 @@
             finish(copies)
         raw = v["raw_s" + here]
         summed = jnp.concatenate([v["full_s" + part][...] for part in parts], axis=1)
-        raw[...] = product(summed, inv[...]) * (1.0 / math.sqrt(rows_first * frames))
+        raw[...] = product(summed, inv[...], HIGH) * (1.0 / math.sqrt(rows_first * frames))
         gram_g, recv_g, across_g, full_g = (
             v[name + here] for name in ("gram_g", "recv_g", "across_g", "full_g")
         )
-        gram_g[...] = cross(raw[...], raw[...])
+        gram_g[...] = cross(raw[...], raw[...], HIGH)
         go_g = halves_out(twin, gram_g, recv_g, v["sem_g" + here])
         last = p + 1 == PASSES
         if last:
@@ -393,13 +413,14 @@
         go_g = halves_across(twin, gram_g, recv_g, across_g, v["sem_h" + here])
         if last:
             first_terms(raw, frames // 4, frames)
-            go_f = scatter("col", col, v["terms_f"], v["recv_f"], v["sem_f"])
         else:
             frame_terms(raw, frames // 2, frames)
             go_r = gather("row", row, sums[...], v["parts_r" + later], v["sem_r" + later])
         finish(go_g)
         full_g[span(twin.core, half), :] = total(across_g)
         go_g = halves_back(twin, full_g, v["sem_i" + here])
+        if last:
+            go_f = scatter("col", col, v["terms_f"], v["recv_f"], v["sem_f"])
         finish(go_g)
         gram = full_g[...] * (1.0 / rows_second)
         down = lax.broadcasted_iota(jnp.int32, (rank, rank), 0)
@@ -410,6 +431,7 @@
         second_gram = gram / wide / tall
     inv[...] = second_gram * frame_gram
     second_out[...] = raw[...] / wide
+    gone = [move(second_out, second_to, 2), move(frames_out, frames_to, 3)]
     invert(inv, 0, steps // 4)
     finish(go_f)
     go_f = gather("col", col, total(v["recv_f"]), v["full_f"], v["sem_f2"])
@@ -417,28 +439,31 @@
     finish(go_f)
     raw = product(v["full_f"][...] / wide, inv[...]) * (1.0 / math.sqrt(rows_second * frames))
     squares = jnp.sum(raw * raw, axis=0, keepdims=True)
-    go_w = gather("row", row, jnp.broadcast_to(squares, (8, rank)), v["parts_w"], v["sem_w"])
+    go_w = spread("row", row, squares, v["parts_w"], v["sem_w"])
     first_out[...] = raw
     finish(go_w)
-    weights = jnp.sqrt(total_blocks(v["parts_w"], row) * (1.0 / rows_first) + epsilon)
-    weights_out[...] = weights
-    first_out[...] = first_out[...] / weights[0:1, :]
+    weights = jnp.sqrt(total(v["parts_w"])[0:1, :] * (1.0 / rows_first) + epsilon)
+    weights_out[...] = jnp.broadcast_to(weights, weights_out.shape)
+    gone.append(move(weights_out, weights_to, 4))
+    first_out[...] = first_out[...] / weights
+    gone.append(move(first_out, first_to, 5))
+    finish(gone)
 
 
 def body(sizes, tensor, initial_first, initial_second):
     frames, own_first, own_second = tensor.shape
     rank = initial_first.shape[1]
     names, scratch = layout(sizes, frames, own_first, own_second, rank)
-    vmem = pl.BlockSpec(memory_space=pltpu.VMEM)
+    anywhere = pl.BlockSpec(memory_space=pl.ANY)
     outs = ((own_first, rank), (own_second, rank), (frames, rank), (8, rank))
     factor_first, second, factor_frames, weights = pl.pallas_call(
         functools.partial(kernel, sizes, names),
         out_shape=[jax.ShapeDtypeStruct(shape, jnp.float32) for shape in outs],
-        in_specs=[pl.BlockSpec(memory_space=pl.ANY), vmem, vmem],
-        out_specs=[vmem] * len(outs),
+        in_specs=[anywhere] * 3,
+        out_specs=[anywhere] * len(outs),
         scratch_shapes=scratch,
         compiler_params=pltpu.CompilerParams(
-            collective_id=0, has_side_effects=True, vmem_limit_bytes=48 * 1024 * 1024
+            collective_id=0, has_side_effects=True, vmem_limit_bytes=67043328
         ),
         name="als",
     )(tensor, initial_first, initial_second)

time: 106 us -> 102 us (0.962)
  Pallas kernels: 98.3 us -> 95.5 us
    pallas_call x1, Pallas kernels: 98.3 us -> 95.5 us  [body(): pl.pallas_call(functools.partial(kernel, sizes, names), out_shape=[jax.Sh...]
    unnamed x9 -> x3, local copies, waits for them, and re-layouts: 6.01 us -> 4.61 us
where the time goes in v2:
time: 102 us
  Pallas kernels  95.5 us (94%)
  local copies, waits for them, and re-layouts  5.87 us (6%)
    pallas_call x1, Pallas kernels, body(): pl.pallas_call(functools.partial(kernel, sizes, names), out_shape=[jax.Sh...  95.5 us
    unnamed x3, local copies, waits for them, and re-layouts  4.61 us

profile of v2, /device:TPU:0, one launch (start us, length us, event | category | flops | bytes accessed | tf_op | source)
XLA Modules:
  0.0 102.0 jit_solution(4345435405440557399)
XLA Ops:
  0.6 95.5 %als.1 = (f32[128,256]{1,0:T(8,128)}, f32[256,256]{1,0:T(8,128)}, f32[32,256]{1,0:T(8,128)}, f32[8,256]{1,0:T(8,128)}) custom-call(f32[32,128,256]{2,1,0:T(8,128)} %tensor.1, f32[128,256]{1,0:T(8,128)} %first_in.1, f32[256,256]{1,0:T(8,128)} %second_in.1), custom_call_target="tpu_custom_call" | custom-call | tf_op jit(solution)/shard_map/als/pallas_call | solution.py:459
  96.1 1.3 %slice.3 = f32[1,256]{1,0:T(1,128)} slice(f32[8,256]{1,0:T(8,128)} %get-tuple-element.11), slice={[0:1], [0:256]} | slice | bytes 2048 | tf_op jit(solution)/shard_map/slice | solution.py:470
  97.4 1.6 %copy.10 = f32[128,256]{1,0:T(8,128)} copy(f32[128,256]{1,0:T(8,128)} %get-tuple-element.16) | data formatting | bytes 262144
  99.0 1.7 %copy.11 = f32[256,256]{1,0:T(8,128)} copy(f32[256,256]{1,0:T(8,128)} %get-tuple-element.17) | data formatting | bytes 524288
  100.6 1.4 %copy.12 = f32[32,256]{1,0:T(8,128)} copy(f32[32,256]{1,0:T(8,128)} %get-tuple-element.18) | data formatting | bytes 65536

commit v3 on v2

--- a/solution.py
+++ b/solution.py
@@ -12,6 +12,7 @@
 LANES = 128
 PIVOTS = 16
 GROUP = 4
+CUTS = 2
 MESH = pl.DeviceIdType.MESH
 HIGHEST = lax.Precision.HIGHEST
 HIGH = lax.Precision.HIGH
@@ -152,6 +153,62 @@
     return [send(here, here, sems, d - 1, {axis: lax.rem(me + d, n)}) for d in range(1, n)]
 
 
+def scatter_piece(n, cut, source, recv, sems):
+    me = lax.axis_index("row")
+    chunk = recv.shape[1]
+    small = chunk // CUTS
+    inside = pl.ds(cut * small, small)
+    copies = []
+    for d in range(1, n):
+        peer = lax.rem(me + d, n)
+        there = pl.ds(pl.multiple_of(peer * chunk + cut * small, 8), small)
+        copies.append(send(
+            source.at[there, :], recv.at[me, inside, :], sems, cut * (n - 1) + d - 1,
+            {"row": peer},
+        ))
+    recv[me, cut * small : (cut + 1) * small, :] = source[
+        pl.ds(pl.multiple_of(me * chunk + cut * small, 8), small), :
+    ]
+    return copies
+
+
+def gather_piece(n, cut, recv, full, sems):
+    me = lax.axis_index("row")
+    chunk = recv.shape[1]
+    small = chunk // CUTS
+    inside = slice(cut * small, (cut + 1) * small)
+    place = pl.ds(pl.multiple_of(me * chunk + cut * small, 8), small)
+    full[place, :] = total(recv[:, inside, :])
+    return [
+        send(
+            full.at[place, :], full.at[place, :], sems, cut * (n - 1) + d - 1,
+            {"row": lax.rem(me + d, n)},
+        )
+        for d in range(1, n)
+    ]
+
+
+def lots_out(sums, lots, recv, sems):
+    n, few = lots.shape[:2]
+    me = lax.axis_index("row")
+    for d in range(n):
+        lots[d] = sums[d * few : (d + 1) * few, :]
+    recv[me] = lots[me]
+    return [
+        send(lots.at[peer], recv.at[me], sems, d, {"row": peer})
+        for d, peer in enumerate(lax.rem(me + e, n) for e in range(1, n))
+    ]
+
+
+def lots_share(axis, n, own, full, sems):
+    me = lax.axis_index(axis)
+    full[me] = own
+    return [
+        send(full.at[me], full.at[me], sems, d - 1, {axis: lax.rem(me + d, n)})
+        for d in range(1, n)
+    ]
+
+
 def finish(copies):
     for copy in copies:
         copy.wait()
@@ -208,12 +265,12 @@
     square = (rank, rank)
     half = rank // 2
     chips = col // 2
+    few = frames // row
+    pieces = CUTS * (row - 1) + 1
     buffers = {
         "tens": (frames, own_first, own_second),
         "held": (frames, own_second, rank),
         "first": (own_first, rank), "second": (own_second, rank),
-        "first_out": (own_first, rank), "second_out": (own_second, rank),
-        "frames_out": (frames, rank), "weights_out": (8, rank),
         "inv": square, "sums": (frames, rank),
         "gram_a": square, "recv_a": (row, half // row, rank), "full_a": square,
         "gram_b": square, "recv_b": (half, rank), "across_b": (chips, half, rank),
@@ -227,13 +284,14 @@
     }
     for p in range(PASSES):
         buffers.update({
-            "parts_r%d" % p: (row * frames, rank), "parts_c%d" % p: (col * frames, rank),
+            "lots_r%d" % p: (row, few, rank), "recv_r%d" % p: (row, few, rank),
+            "parts_c%d" % p: (col, few, rank), "full_r%d" % p: (row, few, rank),
             "raw_s%d" % p: (own_second, rank),
             "gram_g%d" % p: square, "recv_g%d" % p: (half, rank),
             "across_g%d" % p: (chips, half, rank), "full_g%d" % p: square,
         })
         axes.update({
-            "r%d" % p: row, "c%d" % p: col, "g%d" % p: 2, "h%d" % p: chips, "i%d" % p: 2,
+            "r%d" % p: row, "c%d" % p: col, "d%d" % p: row, "g%d" % p: 2, "h%d" % p: chips, "i%d" % p: 2,
         })
         for q in range(rank // LANES):
             buffers.update({
@@ -241,21 +299,20 @@
                 "recv_s%d%d" % (p, q): (row, own_second // row, LANES),
                 "full_s%d%d" % (p, q): (own_second, LANES),
             })
-            axes.update({"s%d%d" % (p, q): row, "t%d%d" % (p, q): row})
+            axes.update({"s%d%d" % (p, q): pieces, "t%d%d" % (p, q): pieces})
     names = list(buffers) + ["sem_" + name for name in axes] + ["sem_load", "sem_move"]
     shapes = [pltpu.VMEM(shape, jnp.float32) for shape in buffers.values()]
     shapes += [pltpu.SemaphoreType.DMA((2, max(n - 1, 1))) for n in axes.values()]
     shapes += [pltpu.SemaphoreType.DMA((frames // math.gcd(frames, GROUP),))]
-    shapes += [pltpu.SemaphoreType.DMA((6,))]
+    shapes += [pltpu.SemaphoreType.DMA((2,))]
     return names, shapes
 
 
-def kernel(sizes, names, tensor, first_in, second_in, first_to, second_to, frames_to, weights_to, *scratch):
+def kernel(sizes, names, tensor, first_in, second_in, first_out, second_out, frames_out, weights_out, *scratch):
     row, col = sizes["row"], sizes["col"]
     v = dict(zip(names, scratch))
     inv, sums, tens, held = v["inv"], v["sums"], v["tens"], v["held"]
-    first, second, frames_out, weights_out = v["first"], v["second"], v["frames_out"], v["weights_out"]
-    first_out, second_out = v["first_out"], v["second_out"]
+    first, second = v["first"], v["second"]
     frames, own_first, own_second = tensor.shape
     rank = first.shape[1]
     half = rank // 2
@@ -321,6 +378,16 @@
 
         lax.fori_loop(0, (stop - start) // group, step, 0)
 
+    def frames_across(name):
+        return lots_share(
+            "col", col, total(v["recv_r" + name]), v["parts_c" + name], v["sem_c" + name]
+        )
+
+    def frames_back(name):
+        return lots_share(
+            "row", row, total(v["parts_c" + name]), v["full_r" + name], v["sem_d" + name]
+        )
+
     def solve_frames(frame_sums):
         raw = product(frame_sums, inv[...]) * (1.0 / math.sqrt(rows_first * rows_second))
         normed = raw / jnp.sqrt(jnp.mean(raw * raw, axis=0, keepdims=True) + epsilon)
@@ -335,23 +402,26 @@
     v["gram_a"][...] = cross(first[...], first[...], HIGH)
     come[1].wait()
     v["gram_b"][...] = cross(second[...], second[...], HIGH)
-    contract(0, loads // 4)
+    contract(0, loads * 5 // 8)
     greeted(sizes)
     offset = twin.core * half
     go_a = scatter("row", row, v["gram_a"], v["recv_a"], v["sem_a"], offset)
     go_b = halves_out(twin, v["gram_b"], v["recv_b"], v["sem_b"])
-    contract(loads // 4, loads * 5 // 8)
+    contract(loads * 5 // 8, loads)
+    go_r = lots_out(sums, v["lots_r0"], v["recv_r0"], v["sem_r0"])
     finish(go_b)
     go_b = halves_across(twin, v["gram_b"], v["recv_b"], v["across_b"], v["sem_b2"])
     finish(go_a)
     go_a = gather("row", row, total(v["recv_a"]), v["full_a"], v["sem_a2"], offset)
-    contract(loads * 5 // 8, loads)
-    go_r = gather("row", row, sums[...], v["parts_r0"], v["sem_r0"])
+    finish(go_r)
+    go_c = frames_across("0")
     finish(go_b)
     v["full_b"][span(twin.core, half), :] = total(v["across_b"])
     go_b = halves_back(twin, v["full_b"], v["sem_b3"])
     finish(go_a)
     go_a = halves_back(twin, v["full_a"], v["sem_a3"])
+    finish(go_c)
+    go_d = frames_back("0")
     finish(go_b)
     finish(go_a)
     first_gram = v["gram_a"]
@@ -360,36 +430,39 @@
     wide = None
     for p in range(PASSES):
         here = str(p)
-        split_at = 0 if p == 0 else steps // 2
         inv[...] = first_gram[...] * second_gram
-        invert(inv, 0, split_at)
-        finish(go_r)
-        go_c = gather(
-            "col", col, total_blocks(v["parts_r" + here], row), v["parts_c" + here],
-            v["sem_c" + here],
-        )
-        invert(inv, split_at, steps)
-        finish(go_c)
-        frame_sums = total_blocks(v["parts_c" + here], col)
+        at = 0
+        if p > 0:
+            at = steps // 4
+            invert(inv, 0, at)
+            finish(go_c)
+            go_d = frames_back(here)
+        invert(inv, at, steps)
+        finish(go_d)
+        full_r = v["full_r" + here]
+        frame_sums = jnp.concatenate([full_r[d] for d in range(row)], axis=0)
         if wide is not None:
             frame_sums = frame_sums / wide
         frame_gram = solve_frames(frame_sums)
         parts = [here + str(q) for q in range(tiles)]
+        pieces = [(part, cut) for part in parts for cut in range(CUTS)]
         go_s = []
         for q, part in enumerate(parts):
             second_terms(v["terms_s" + part], q)
-            go_s.append(scatter(
-                "row", row, v["terms_s" + part], v["recv_s" + part], v["sem_s" + part]
-            ))
+            for cut in range(CUTS):
+                go_s.append(scatter_piece(
+                    row, cut, v["terms_s" + part], v["recv_s" + part], v["sem_s" + part]
+                ))
         inv[...] = first_gram[...] * frame_gram
         go_t = []
         at = 0
-        for q, part in enumerate(parts):
-            invert(inv, at, steps * (5 + 2 * q) // 8)
-            at = steps * (5 + 2 * q) // 8
+        for q, (part, cut) in enumerate(pieces):
+            until = min(steps, steps * 5 // 8 + q * steps // (2 * len(pieces)))
+            invert(inv, at, until)
+            at = until
             finish(go_s[q])
-            go_t.append(gather(
-                "row", row, total(v["recv_s" + part]), v["full_s" + part], v["sem_t" + part]
+            go_t.append(gather_piece(
+                row, cut, v["recv_s" + part], v["full_s" + part], v["sem_t" + part]
             ))
         invert(inv, at, steps)
         for copies in go_t:
@@ -415,8 +488,11 @@
             first_terms(raw, frames // 4, frames)
         else:
             frame_terms(raw, frames // 2, frames)
-            go_r = gather("row", row, sums[...], v["parts_r" + later], v["sem_r" + later])
+            go_r = lots_out(sums, v["lots_r" + later], v["recv_r" + later], v["sem_r" + later])
         finish(go_g)
+        if not last:
+            finish(go_r)
+            go_c = frames_across(later)
         full_g[span(twin.core, half), :] = total(across_g)
         go_g = halves_back(twin, full_g, v["sem_i" + here])
         if last:
@@ -431,7 +507,6 @@
         second_gram = gram / wide / tall
     inv[...] = second_gram * frame_gram
     second_out[...] = raw[...] / wide
-    gone = [move(second_out, second_to, 2), move(frames_out, frames_to, 3)]
     invert(inv, 0, steps // 4)
     finish(go_f)
     go_f = gather("col", col, total(v["recv_f"]), v["full_f"], v["sem_f2"])
@@ -443,31 +518,56 @@
     first_out[...] = raw
     finish(go_w)
     weights = jnp.sqrt(total(v["parts_w"])[0:1, :] * (1.0 / rows_first) + epsilon)
-    weights_out[...] = jnp.broadcast_to(weights, weights_out.shape)
-    gone.append(move(weights_out, weights_to, 4))
+    weights_out[...] = weights
     first_out[...] = first_out[...] / weights
-    gone.append(move(first_out, first_to, 5))
-    finish(gone)
+
+
+def deliver(*refs):
+    half = len(refs) // 2
+    sems = refs[-1]
+    copies = [
+        pltpu.make_async_copy(source, target, sems.at[k])
+        for k, (source, target) in enumerate(zip(refs[:half], refs[half : 2 * half]))
+    ]
+    for copy in copies:
+        copy.start()
+    for copy in copies:
+        copy.wait()
 
 
 def body(sizes, tensor, initial_first, initial_second):
     frames, own_first, own_second = tensor.shape
     rank = initial_first.shape[1]
     names, scratch = layout(sizes, frames, own_first, own_second, rank)
-    anywhere = pl.BlockSpec(memory_space=pl.ANY)
-    outs = ((own_first, rank), (own_second, rank), (frames, rank), (8, rank))
-    factor_first, second, factor_frames, weights = pl.pallas_call(
+    far = pl.BlockSpec(memory_space=pltpu.HBM)
+    near = pl.BlockSpec(memory_space=pltpu.VMEM)
+    outs = ((own_first, rank), (own_second, rank), (frames, rank), (1, rank))
+    shapes = [jax.ShapeDtypeStruct(shape, jnp.float32) for shape in outs]
+    results = pl.pallas_call(
         functools.partial(kernel, sizes, names),
-        out_shape=[jax.ShapeDtypeStruct(shape, jnp.float32) for shape in outs],
-        in_specs=[anywhere] * 3,
-        out_specs=[anywhere] * len(outs),
+        out_shape=shapes,
+        in_specs=[far] * 3,
+        out_specs=[near] * len(outs),
         scratch_shapes=scratch,
         compiler_params=pltpu.CompilerParams(
-            collective_id=0, has_side_effects=True, vmem_limit_bytes=67043328
+            collective_id=0, has_side_effects=True, vmem_limit_bytes=48 * 1024 * 1024
         ),
         name="als",
-    )(tensor, initial_first, initial_second)
-    return (factor_first, second, factor_frames, weights[0])
+    )(*[
+        pltpu.with_memory_space_constraint(x, pltpu.HBM)
+        for x in (tensor, initial_first, initial_second)
+    ])
+    results = pl.pallas_call(
+        deliver,
+        out_shape=shapes,
+        in_specs=[near] * len(outs),
+        out_specs=[far] * len(outs),
+        scratch_shapes=[pltpu.SemaphoreType.DMA((len(outs),))],
+        compiler_params=pltpu.CompilerParams(vmem_limit_bytes=1024 * 1024),
+        name="deliver",
+    )(*results)
+    factor_first, second, factor_frames, weights = results
+    return (factor_first, second, factor_frames, weights.reshape(rank))
 
 
 def solution(mesh):

time: 102 us -> 96.6 us (0.947)
  local copies, waits for them, and re-layouts: 5.87 us -> 0 us
    unnamed x3 -> x0, local copies, waits for them, and re-layouts: 4.61 us -> none
    slice x1 -> x0, local copies, waits for them, and re-layouts: 1.26 us -> none  [body(): return (factor_first, second, factor_frames, weights[0])]
    pallas_call x1 -> x2, Pallas kernels: 95.5 us -> 95.8 us  [the longest x1 95 us: body(): pl.pallas_call(functools.partial(kernel, sizes, names), out_shape=shapes,...]
where the time goes in v3:
time: 96.6 us; the launch traced here: 96.5 us
  Pallas kernels  95.8 us (99%)
    pallas_call x1, Pallas kernels, body(): pl.pallas_call(functools.partial(kernel, sizes, names), out_shape=shapes,...  95 us

profile of v3, /device:TPU:0, one launch (start us, length us, event | category | flops | bytes accessed | tf_op | source)
XLA Modules:
  0.0 96.5 jit_solution(3248350292100064765)
XLA Ops:
  0.6 95.0 %als.1 = (f32[128,256]{1,0:T(8,128)S(1)}, f32[256,256]{1,0:T(8,128)S(1)}, f32[32,256]{1,0:T(8,128)S(1)}, f32[1,256]{1,0:T(1,128)S(1)}) custom-call(f32[32,128,256]{2,1,0:T(8,128)} %tensor.1, f32[128,256]{1,0:T(8,128)} %first_in.1, f32[256,256]{1,0:T(8,128)} %second_in.1), custom_call_target="tpu_custom_call" | custom-call | tf_op jit(solution)/shard_map/als/pallas_call | solution.py:546
  95.7 0.8 deliver.1

commit v4 on v3

--- a/solution.py
+++ b/solution.py
@@ -37,63 +37,94 @@
     return high, mid, (rest - mid.astype(jnp.float32)).astype(jnp.bfloat16)
 
 
-def outer(left, right):
-    h, m, l = split(left)
-    hh, mm, ll = split(right)
-    return lax.dot_general(
-        jnp.concatenate([h, h, m, h, m, l], axis=0),
-        jnp.concatenate([hh, mm, hh, ll, mm, hh], axis=0),
-        (((0,), (0,)), ((), ())), preferred_element_type=jnp.float32,
-    )
-
-
-def invert(a, start, stop):
+def stacked(solved):
+    h, m, l = split(solved[...])
+    return jnp.concatenate([h, m, h, l, m, h], axis=0)
+
+
+def update(left, right):
+    return jnp.dot(left, right, preferred_element_type=jnp.float32)
+
+
+def begin(a, panel, solved, left):
+    panel[...] = a[0:PIVOTS, :]
+    solved[...] = jnp.zeros_like(solved)
+    left[...] = jnp.zeros_like(left)
+
+
+def flush(a, panel, solved, left):
+    a[...] = a[...] - update(left[...], stacked(solved))
+    a[a.shape[0] - PIVOTS :, :] = solved[...]
+
+
+def invert(a, panel, solved, left, start, stop):
     size = a.shape[0]
     tiles = size // LANES
+    each = LANES // PIVOTS
     row = lax.broadcasted_iota(jnp.int32, (PIVOTS, LANES), 0)
-    lanes = [
-        lax.broadcasted_iota(jnp.int32, (PIVOTS, LANES), 1) + q * LANES for q in range(tiles)
-    ]
-    wide = lax.broadcasted_iota(jnp.int32, (PIVOTS, size), 1)
-    whole = lax.broadcasted_iota(jnp.int32, (size, size), 1)
-
-    def step(g, carry):
-        base = g * PIVOTS
-        here = pl.ds(pl.multiple_of(base, PIVOTS), PIVOTS)
-        rows = [a[here, q * LANES : (q + 1) * LANES] for q in range(tiles)]
-        cols = []
+    lane = lax.broadcasted_iota(jnp.int32, (PIVOTS, LANES), 1)
+    across = lax.broadcasted_iota(jnp.int32, (size, LANES), 1)
+    parts = [slice(q * LANES, (q + 1) * LANES) for q in range(tiles)]
+
+    def line(x, t):
+        return jnp.broadcast_to(x[t : t + 1, :], (PIVOTS, LANES))
+
+    def block(g):
+        return pl.ds(pl.multiple_of(g * PIVOTS, PIVOTS), PIVOTS)
+
+    def step(own, g, carry):
+        at = g * PIVOTS - own * LANES
+        place = lane - at
+        inside = (place >= 0) & (place < PIVOTS)
+
+        def columns(x):
+            picked = [jnp.where(place == t, x, 0.0) for t in range(PIVOTS)]
+            return [
+                jnp.broadcast_to(jnp.sum(y, axis=1, keepdims=True), (PIVOTS, LANES))
+                for y in picked
+            ]
+
+        rows = [panel[:, part] for part in parts]
+        cols = columns(rows[own])
+        right = stacked(solved)
+        ahead = block(jnp.minimum(g + 1, size // PIVOTS - 1))
+        stale = a[ahead, :] - update(left[ahead, :], right)
+        stale = [stale[:, part] for part in parts]
+        scales = columns(stale[own])
+        stale[own] = jnp.where(inside, 0.0, stale[own])
+        whole = update(left[...], right)
+        behind = block(jnp.maximum(g - 1, 0))
+        for q, part in enumerate(parts):
+            kept, done = a[:, part] - whole[:, part], solved[:, part]
+            if q == own:
+                kept = jnp.where((across >= at) & (across < at + PIVOTS), 0.0, kept)
+                done = jnp.where(inside, 0.0, done)
+            a[:, part] = kept
+            a[behind, part] = done
+        beside = jnp.where(inside, 0.0, jnp.where(place < 0, -rows[own], rows[own]))
+        h, m, l = split(
+            jnp.concatenate([-x for x in rows[:own]] + [beside] + rows[own + 1 :], axis=1)
+        )
+        left[...] = jnp.concatenate([h, h, m, h, m, l], axis=0).T
+        work = list(rows)
+        work[own] = jnp.where(inside, jnp.where(place == row, 1.0, 0.0), rows[own])
         for t in range(PIVOTS):
-            picked = sum(jnp.where(lanes[q] == base + t, rows[q], 0.0) for q in range(tiles))
-            cols.append(
-                jnp.broadcast_to(jnp.sum(picked, axis=1, keepdims=True), (PIVOTS, LANES))
-            )
-        work = []
-        for q in range(tiles):
-            place = lanes[q] - base
-            inside = (place >= 0) & (place < PIVOTS)
-            unit = jnp.where(place == row, 1.0, 0.0)
-            work.append(jnp.where(inside, unit, rows[q]))
-        for t in range(PIVOTS):
-            pivot = 1.0 / jnp.broadcast_to(cols[t][t : t + 1, :], (PIVOTS, LANES))
-            at = row == t
-
-            def reduced(x):
-                scaled = jnp.broadcast_to(x[t : t + 1, :], (PIVOTS, LANES)) * pivot
-                return jnp.where(at, scaled, x - cols[t] * scaled)
-
-            later = [reduced(cols[s]) for s in range(t + 1, PIVOTS)]
-            work = [reduced(w) for w in work]
-            cols[t + 1 :] = later
-        solved = jnp.concatenate(work, axis=1)
-        raw = a[here, :]
-        inside = (wide >= base) & (wide < base + PIVOTS)
-        left = jnp.where(inside, 0.0, jnp.where(wide < base, -raw, raw))
-        kept = jnp.where((whole >= base) & (whole < base + PIVOTS), 0.0, a[...])
-        a[...] = kept - outer(left, solved)
-        a[here, :] = solved
+            pivot = 1.0 / line(cols[t], t)
+            factor = (cols[t] - jnp.where(row == t, 1.0, 0.0)) * pivot
+            cols[t + 1 :] = [x - factor * line(x, t) for x in cols[t + 1 :]]
+            work = [x - factor * line(x, t) for x in work]
+        for q, part in enumerate(parts):
+            fresh = stale[q]
+            for t in range(PIVOTS):
+                fresh = fresh - scales[t] * line(work[q], t)
+            panel[:, part] = fresh
+            solved[:, part] = work[q]
         return carry
 
-    lax.fori_loop(start, stop, step, 0)
+    for q in range(tiles):
+        low, high = max(start, q * each), min(stop, (q + 1) * each)
+        if low < high:
+            lax.fori_loop(low, high, functools.partial(step, q), 0)
 
 
 def greet(sizes):
@@ -271,7 +302,8 @@
         "tens": (frames, own_first, own_second),
         "held": (frames, own_second, rank),
         "first": (own_first, rank), "second": (own_second, rank),
-        "inv": square, "sums": (frames, rank),
+        "inv": square, "panel": (PIVOTS, rank), "solved": (PIVOTS, rank),
+        "sums": (frames, rank),
         "gram_a": square, "recv_a": (row, half // row, rank), "full_a": square,
         "gram_b": square, "recv_b": (half, rank), "across_b": (chips, half, rank),
         "full_b": square,
@@ -302,6 +334,8 @@
             axes.update({"s%d%d" % (p, q): pieces, "t%d%d" % (p, q): pieces})
     names = list(buffers) + ["sem_" + name for name in axes] + ["sem_load", "sem_move"]
     shapes = [pltpu.VMEM(shape, jnp.float32) for shape in buffers.values()]
+    names.insert(len(shapes), "across_left")
+    shapes.append(pltpu.VMEM((rank, 6 * PIVOTS), jnp.bfloat16))
     shapes += [pltpu.SemaphoreType.DMA((2, max(n - 1, 1))) for n in axes.values()]
     shapes += [pltpu.SemaphoreType.DMA((frames // math.gcd(frames, GROUP),))]
     shapes += [pltpu.SemaphoreType.DMA((2,))]
@@ -388,11 +422,22 @@
             "row", row, total(v["parts_c" + name]), v["full_r" + name], v["sem_d" + name]
         )
 
-    def solve_frames(frame_sums):
-        raw = product(frame_sums, inv[...]) * (1.0 / math.sqrt(rows_first * rows_second))
+    def solve_frames(frame_sums, scale):
+        raw = product(frame_sums * scale, inv[...]) * scale
+        raw = raw * (1.0 / math.sqrt(rows_first * rows_second))
         normed = raw / jnp.sqrt(jnp.mean(raw * raw, axis=0, keepdims=True) + epsilon)
         frames_out[...] = normed
         return cross(normed, normed) / frames
+
+    state = (inv, v["panel"], v["solved"], v["across_left"])
+
+    def unit(gram):
+        down = lax.broadcasted_iota(jnp.int32, (rank, rank), 0)
+        across = lax.broadcasted_iota(jnp.int32, (rank, rank), 1)
+        diagonal = jnp.where(down == across, gram, 0.0)
+        wide = 1.0 / jnp.sqrt(jnp.sum(diagonal, axis=0, keepdims=True))
+        tall = 1.0 / jnp.sqrt(jnp.sum(diagonal, axis=1, keepdims=True))
+        return gram * wide * tall, wide
 
     greet(sizes)
     come = [move(first_in, first, 0), move(second_in, second, 1)]
@@ -400,50 +445,50 @@
         load(g).start()
     come[0].wait()
     v["gram_a"][...] = cross(first[...], first[...], HIGH)
-    come[1].wait()
-    v["gram_b"][...] = cross(second[...], second[...], HIGH)
-    contract(0, loads * 5 // 8)
     greeted(sizes)
     offset = twin.core * half
     go_a = scatter("row", row, v["gram_a"], v["recv_a"], v["sem_a"], offset)
+    come[1].wait()
+    v["gram_b"][...] = cross(second[...], second[...], HIGH)
     go_b = halves_out(twin, v["gram_b"], v["recv_b"], v["sem_b"])
-    contract(loads * 5 // 8, loads)
-    go_r = lots_out(sums, v["lots_r0"], v["recv_r0"], v["sem_r0"])
+    contract(0, loads // 2)
     finish(go_b)
     go_b = halves_across(twin, v["gram_b"], v["recv_b"], v["across_b"], v["sem_b2"])
+    contract(loads // 2, loads)
+    go_r = lots_out(sums, v["lots_r0"], v["recv_r0"], v["sem_r0"])
     finish(go_a)
     go_a = gather("row", row, total(v["recv_a"]), v["full_a"], v["sem_a2"], offset)
+    finish(go_b)
+    v["full_b"][span(twin.core, half), :] = total(v["across_b"])
+    go_b = halves_back(twin, v["full_b"], v["sem_b3"])
     finish(go_r)
     go_c = frames_across("0")
     finish(go_b)
-    v["full_b"][span(twin.core, half), :] = total(v["across_b"])
-    go_b = halves_back(twin, v["full_b"], v["sem_b3"])
+    second_gram, second_scale = unit(v["full_b"][...] * (1.0 / rows_second))
     finish(go_a)
     go_a = halves_back(twin, v["full_a"], v["sem_a3"])
-    finish(go_c)
-    go_d = frames_back("0")
-    finish(go_b)
     finish(go_a)
     first_gram = v["gram_a"]
-    first_gram[...] = v["full_a"][...] * (1.0 / rows_first)
-    second_gram = v["full_b"][...] * (1.0 / rows_second)
+    first_gram[...], first_scale = unit(v["full_a"][...] * (1.0 / rows_first))
     wide = None
     for p in range(PASSES):
         here = str(p)
         inv[...] = first_gram[...] * second_gram
-        at = 0
-        if p > 0:
-            at = steps // 4
-            invert(inv, 0, at)
-            finish(go_c)
-            go_d = frames_back(here)
-        invert(inv, at, steps)
+        begin(*state)
+        invert(*state, 0, steps // 8)
+        finish(go_c)
+        go_d = frames_back(here)
+        invert(*state, steps // 8, steps)
+        flush(*state)
         finish(go_d)
         full_r = v["full_r" + here]
         frame_sums = jnp.concatenate([full_r[d] for d in range(row)], axis=0)
-        if wide is not None:
+        if wide is None:
+            frame_scale = first_scale * second_scale
+        else:
             frame_sums = frame_sums / wide
-        frame_gram = solve_frames(frame_sums)
+            frame_scale = first_scale
+        frame_gram = solve_frames(frame_sums, frame_scale)
         parts = [here + str(q) for q in range(tiles)]
         pieces = [(part, cut) for part in parts for cut in range(CUTS)]
         go_s = []
@@ -456,20 +501,24 @@
         inv[...] = first_gram[...] * frame_gram
         go_t = []
         at = 0
+        begin(*state)
         for q, (part, cut) in enumerate(pieces):
-            until = min(steps, steps * 5 // 8 + q * steps // (2 * len(pieces)))
-            invert(inv, at, until)
-            at = until
+            until = steps * 7 // 8 if q == 0 else steps
+            if at < until:
+                invert(*state, at, until)
+                at = until
             finish(go_s[q])
             go_t.append(gather_piece(
                 row, cut, v["recv_s" + part], v["full_s" + part], v["sem_t" + part]
             ))
-        invert(inv, at, steps)
+        flush(*state)
         for copies in go_t:
             finish(copies)
         raw = v["raw_s" + here]
         summed = jnp.concatenate([v["full_s" + part][...] for part in parts], axis=1)
-        raw[...] = product(summed, inv[...], HIGH) * (1.0 / math.sqrt(rows_first * frames))
+        raw[...] = product(summed * first_scale, inv[...], HIGH) * (
+            first_scale * (1.0 / math.sqrt(rows_first * frames))
+        )
         gram_g, recv_g, across_g, full_g = (
             v[name + here] for name in ("gram_g", "recv_g", "across_g", "full_g")
         )
@@ -481,18 +530,16 @@
             first_terms(raw, 0, frames // 4)
         else:
             later = str(p + 1)
-            frame_terms(raw, 0, frames // 2)
+            frame_terms(raw, 0, frames)
+            go_r = lots_out(sums, v["lots_r" + later], v["recv_r" + later], v["sem_r" + later])
         finish(go_g)
         go_g = halves_across(twin, gram_g, recv_g, across_g, v["sem_h" + here])
         if last:
             first_terms(raw, frames // 4, frames)
         else:
-            frame_terms(raw, frames // 2, frames)
-            go_r = lots_out(sums, v["lots_r" + later], v["recv_r" + later], v["sem_r" + later])
-        finish(go_g)
-        if not last:
             finish(go_r)
             go_c = frames_across(later)
+        finish(go_g)
         full_g[span(twin.core, half), :] = total(across_g)
         go_g = halves_back(twin, full_g, v["sem_i" + here])
         if last:
@@ -507,10 +554,12 @@
         second_gram = gram / wide / tall
     inv[...] = second_gram * frame_gram
     second_out[...] = raw[...] / wide
-    invert(inv, 0, steps // 4)
+    begin(*state)
+    invert(*state, 0, steps // 2)
     finish(go_f)
     go_f = gather("col", col, total(v["recv_f"]), v["full_f"], v["sem_f2"])
-    invert(inv, steps // 4, steps)
+    invert(*state, steps // 2, steps)
+    flush(*state)
     finish(go_f)
     raw = product(v["full_f"][...] / wide, inv[...]) * (1.0 / math.sqrt(rows_second * frames))
     squares = jnp.sum(raw * raw, axis=0, keepdims=True)

time: 96.6 us -> 89.8 us (0.930)
  Pallas kernels: 95.8 us -> 89 us
    pallas_call x1, Pallas kernels: 95 us -> 88.2 us  [body(): pl.pallas_call(functools.partial(kernel, sizes, names), out_shape=shapes,...]
where the time goes in v4:
time: 89.8 us; the launch traced here: 89.6 us
  Pallas kernels  89 us (99%)
    pallas_call x1, Pallas kernels, body(): pl.pallas_call(functools.partial(kernel, sizes, names), out_shape=shapes,...  88.2 us

profile of v4, /device:TPU:0, one launch (start us, length us, event | category | flops | bytes accessed | tf_op | source)
XLA Modules:
  0.0 89.6 jit_solution(8748810603829450849)
XLA Ops:
  0.6 88.2 %als.1 = (f32[128,256]{1,0:T(8,128)S(1)}, f32[256,256]{1,0:T(8,128)S(1)}, f32[32,256]{1,0:T(8,128)S(1)}, f32[1,256]{1,0:T(1,128)S(1)}) custom-call(f32[32,128,256]{2,1,0:T(8,128)} %tensor.1, f32[128,256]{1,0:T(8,128)} %first_in.1, f32[256,256]{1,0:T(8,128)} %second_in.1), custom_call_target="tpu_custom_call" | custom-call | tf_op jit(solution)/shard_map/als/pallas_call | solution.py:595
  88.8 0.8 deliver.1

commit v5 on v4

--- a/solution.py
+++ b/solution.py
@@ -141,29 +141,40 @@
     pl.semaphore_wait(pltpu.get_barrier_semaphore(), sum(n - 1 for n in sizes.values()))
 
 
-def send(source, target, sems, at, device):
-    copy = pltpu.make_async_remote_copy(
-        src_ref=source, dst_ref=target, send_sem=sems.at[0, at], recv_sem=sems.at[1, at],
+def send(source, target, sems, device):
+    pltpu.make_async_remote_copy(
+        src_ref=source, dst_ref=target, send_sem=sems.at[0], recv_sem=sems.at[1],
         device_id=device, device_id_type=MESH,
-    )
-    copy.start()
-    return copy
+    ).start()
+
+
+def finish(exchange):
+    view, sems = exchange
+    if view is not None:
+        for k in range(2):
+            pltpu.make_async_copy(view, view, sems.at[k]).wait()
 
 
 def span(index, chunk):
     return pl.ds(pl.multiple_of(index * chunk, 8), chunk)
+
+
+def others(axis, n):
+    me = lax.axis_index(axis)
+    return [lax.rem(me + d, n) for d in range(1, n)]
 
 
 def scatter(axis, n, source, recv, sems, offset=0):
     me = lax.axis_index(axis)
     chunk = recv.shape[1]
-    copies = []
-    for d in range(1, n):
-        peer = lax.rem(me + d, n)
-        there = pl.ds(pl.multiple_of(offset + peer * chunk, 8), chunk)
-        copies.append(send(source.at[there, :], recv.at[me], sems, d - 1, {axis: peer}))
-    recv[me] = source[pl.ds(pl.multiple_of(offset + me * chunk, 8), chunk), :]
-    return copies
+
+    def of(peer):
+        return pl.ds(pl.multiple_of(offset + peer * chunk, 8), chunk)
+
+    for peer in others(axis, n):
+        send(source.at[of(peer), :], recv.at[me], sems, {axis: peer})
+    recv[me] = source[of(me), :]
+    return recv.at[pl.ds(0, n - 1)], sems
 
 
 def gather(axis, n, own, full, sems, offset=0):
@@ -171,17 +182,18 @@
     chunk = own.shape[0]
     place = pl.ds(pl.multiple_of(offset + me * chunk, 8), chunk)
     full[place, :] = own
-    return [
-        send(full.at[place, :], full.at[place, :], sems, d - 1, {axis: lax.rem(me + d, n)})
-        for d in range(1, n)
-    ]
+    for peer in others(axis, n):
+        send(full.at[place, :], full.at[place, :], sems, {axis: peer})
+    return full.at[pl.ds(0, (n - 1) * chunk), :], sems
 
 
 def spread(axis, n, line, parts, sems):
     me = lax.axis_index(axis)
-    here = parts.at[me, pl.ds(0, 1), :]
+    one = pl.ds(0, 1)
     parts[me, 0:1, :] = line
-    return [send(here, here, sems, d - 1, {axis: lax.rem(me + d, n)}) for d in range(1, n)]
+    for peer in others(axis, n):
+        send(parts.at[me, one, :], parts.at[me, one, :], sems, {axis: peer})
+    return parts.at[pl.ds(0, n - 1), one, :], sems
 
 
 def scatter_piece(n, cut, source, recv, sems):
@@ -189,18 +201,14 @@
     chunk = recv.shape[1]
     small = chunk // CUTS
     inside = pl.ds(cut * small, small)
-    copies = []
-    for d in range(1, n):
-        peer = lax.rem(me + d, n)
-        there = pl.ds(pl.multiple_of(peer * chunk + cut * small, 8), small)
-        copies.append(send(
-            source.at[there, :], recv.at[me, inside, :], sems, cut * (n - 1) + d - 1,
-            {"row": peer},
-        ))
-    recv[me, cut * small : (cut + 1) * small, :] = source[
-        pl.ds(pl.multiple_of(me * chunk + cut * small, 8), small), :
-    ]
-    return copies
+
+    def of(peer):
+        return pl.ds(pl.multiple_of(peer * chunk + cut * small, 8), small)
+
+    for peer in others("row", n):
+        send(source.at[of(peer), :], recv.at[me, inside, :], sems.at[cut], {"row": peer})
+    recv[me, cut * small : (cut + 1) * small, :] = source[of(me), :]
+    return recv.at[pl.ds(0, n - 1), inside, :], sems.at[cut]
 
 
 def gather_piece(n, cut, recv, full, sems):
@@ -210,13 +218,9 @@
     inside = slice(cut * small, (cut + 1) * small)
     place = pl.ds(pl.multiple_of(me * chunk + cut * small, 8), small)
     full[place, :] = total(recv[:, inside, :])
-    return [
-        send(
-            full.at[place, :], full.at[place, :], sems, cut * (n - 1) + d - 1,
-            {"row": lax.rem(me + d, n)},
-        )
-        for d in range(1, n)
-    ]
+    for peer in others("row", n):
+        send(full.at[place, :], full.at[place, :], sems.at[cut], {"row": peer})
+    return full.at[pl.ds(0, (n - 1) * small), :], sems.at[cut]
 
 
 def lots_out(sums, lots, recv, sems):
@@ -225,24 +229,17 @@
     for d in range(n):
         lots[d] = sums[d * few : (d + 1) * few, :]
     recv[me] = lots[me]
-    return [
-        send(lots.at[peer], recv.at[me], sems, d, {"row": peer})
-        for d, peer in enumerate(lax.rem(me + e, n) for e in range(1, n))
-    ]
+    for peer in others("row", n):
+        send(lots.at[peer], recv.at[me], sems, {"row": peer})
+    return recv.at[pl.ds(0, n - 1)], sems
 
 
 def lots_share(axis, n, own, full, sems):
     me = lax.axis_index(axis)
     full[me] = own
-    return [
-        send(full.at[me], full.at[me], sems, d - 1, {axis: lax.rem(me + d, n)})
-        for d in range(1, n)
-    ]
-
-
-def finish(copies):
-    for copy in copies:
-        copy.wait()
+    for peer in others(axis, n):
+        send(full.at[me], full.at[me], sems, {axis: peer})
+    return full.at[pl.ds(0, n - 1)], sems
 
 
 def total(recv):
@@ -275,20 +272,25 @@
 
 def halves_out(twin, gram, recv, sems):
     half = gram.shape[0] // 2
-    return [send(gram.at[span(1 - twin.core, half), :], recv, sems, 0, twin.partner)]
+    send(gram.at[span(1 - twin.core, half), :], recv, sems, twin.partner)
+    return recv, sems
 
 
 def halves_across(twin, gram, recv, across, sems):
     half = gram.shape[0] // 2
     across[twin.chip] = gram[span(twin.core, half), :] + recv[...]
     here = across.at[twin.chip]
-    return [send(here, here, sems, d, peer) for d, peer in enumerate(twin.others)]
+    for peer in twin.others:
+        send(here, here, sems, peer)
+    view = across.at[pl.ds(0, twin.count - 1)] if twin.count > 1 else None
+    return view, sems
 
 
 def halves_back(twin, full, sems):
     half = full.shape[0] // 2
     mine = full.at[span(twin.core, half), :]
-    return [send(mine, mine, sems, 0, twin.partner)]
+    send(mine, mine, sems, twin.partner)
+    return mine, sems
 
 
 def layout(sizes, frames, own_first, own_second, rank):
@@ -297,7 +299,6 @@
     half = rank // 2
     chips = col // 2
     few = frames // row
-    pieces = CUTS * (row - 1) + 1
     buffers = {
         "tens": (frames, own_first, own_second),
         "held": (frames, own_second, rank),
@@ -310,10 +311,8 @@
         "terms_f": (own_first, rank), "recv_f": (col, own_first // col, rank),
         "full_f": (own_first, rank), "parts_w": (row, 8, rank),
     }
-    axes = {
-        "a": row, "a2": row, "a3": 2, "b": 2, "b2": chips, "b3": 2, "f": col, "f2": col,
-        "w": row,
-    }
+    pairs = ["a", "a2", "a3", "b", "b2", "b3", "f", "f2", "w"]
+    cuts = []
     for p in range(PASSES):
         buffers.update({
             "lots_r%d" % p: (row, few, rank), "recv_r%d" % p: (row, few, rank),
@@ -322,21 +321,20 @@
             "gram_g%d" % p: square, "recv_g%d" % p: (half, rank),
             "across_g%d" % p: (chips, half, rank), "full_g%d" % p: square,
         })
-        axes.update({
-            "r%d" % p: row, "c%d" % p: col, "d%d" % p: row, "g%d" % p: 2, "h%d" % p: chips, "i%d" % p: 2,
-        })
+        pairs += [name + str(p) for name in "rcdghi"]
         for q in range(rank // LANES):
             buffers.update({
                 "terms_s%d%d" % (p, q): (own_second, LANES),
                 "recv_s%d%d" % (p, q): (row, own_second // row, LANES),
                 "full_s%d%d" % (p, q): (own_second, LANES),
             })
-            axes.update({"s%d%d" % (p, q): pieces, "t%d%d" % (p, q): pieces})
-    names = list(buffers) + ["sem_" + name for name in axes] + ["sem_load", "sem_move"]
+            cuts += ["s%d%d" % (p, q), "t%d%d" % (p, q)]
+    names = list(buffers) + ["sem_" + name for name in pairs + cuts] + ["sem_load", "sem_move"]
     shapes = [pltpu.VMEM(shape, jnp.float32) for shape in buffers.values()]
     names.insert(len(shapes), "across_left")
     shapes.append(pltpu.VMEM((rank, 6 * PIVOTS), jnp.bfloat16))
-    shapes += [pltpu.SemaphoreType.DMA((2, max(n - 1, 1))) for n in axes.values()]
+    shapes += [pltpu.SemaphoreType.DMA((2,)) for name in pairs]
+    shapes += [pltpu.SemaphoreType.DMA((CUTS, 2)) for name in cuts]
     shapes += [pltpu.SemaphoreType.DMA((frames // math.gcd(frames, GROUP),))]
     shapes += [pltpu.SemaphoreType.DMA((2,))]
     return names, shapes
@@ -439,11 +437,12 @@
         tall = 1.0 / jnp.sqrt(jnp.sum(diagonal, axis=1, keepdims=True))
         return gram * wide * tall, wide
 
+    come = [move(first_in, first, 0)]
     greet(sizes)
-    come = [move(first_in, first, 0), move(second_in, second, 1)]
+    come.append(move(second_in, second, 1))
+    come[0].wait()
     for g in range(loads):
         load(g).start()
-    come[0].wait()
     v["gram_a"][...] = cross(first[...], first[...], HIGH)
     greeted(sizes)
     offset = twin.core * half
@@ -512,8 +511,8 @@
                 row, cut, v["recv_s" + part], v["full_s" + part], v["sem_t" + part]
             ))
         flush(*state)
-        for copies in go_t:
-            finish(copies)
+        for go in go_t:
+            finish(go)
         raw = v["raw_s" + here]
         summed = jnp.concatenate([v["full_s" + part][...] for part in parts], axis=1)
         raw[...] = product(summed * first_scale, inv[...], HIGH) * (
@@ -536,14 +535,13 @@
         go_g = halves_across(twin, gram_g, recv_g, across_g, v["sem_h" + here])
         if last:
             first_terms(raw, frames // 4, frames)
+            go_f = scatter("col", col, v["terms_f"], v["recv_f"], v["sem_f"])
         else:
             finish(go_r)
             go_c = frames_across(later)
         finish(go_g)
         full_g[span(twin.core, half), :] = total(across_g)
         go_g = halves_back(twin, full_g, v["sem_i" + here])
-        if last:
-            go_f = scatter("col", col, v["terms_f"], v["recv_f"], v["sem_f"])
         finish(go_g)
         gram = full_g[...] * (1.0 / rows_second)
         down = lax.broadcasted_iota(jnp.int32, (rank, rank), 0)

time: 89.8 us -> 87.6 us (0.976)
  Pallas kernels: 89 us -> 86.8 us
    pallas_call x1, Pallas kernels: 88.2 us -> 86 us  [body(): pl.pallas_call(functools.partial(kernel, sizes, names), out_shape=shapes,...]
where the time goes in v5:
time: 87.6 us; the launch traced here: 87.4 us
  Pallas kernels  86.8 us (99%)
    pallas_call x1, Pallas kernels, body(): pl.pallas_call(functools.partial(kernel, sizes, names), out_shape=shapes,...  86 us

profile of v5, /device:TPU:0, one launch (start us, length us, event | category | flops | bytes accessed | tf_op | source)
XLA Modules:
  0.0 87.4 jit_solution(11083271544617271459)
XLA Ops:
  0.6 86.0 %als.1 = (f32[128,256]{1,0:T(8,128)S(1)}, f32[256,256]{1,0:T(8,128)S(1)}, f32[32,256]{1,0:T(8,128)S(1)}, f32[1,256]{1,0:T(1,128)S(1)}) custom-call(f32[32,128,256]{2,1,0:T(8,128)} %tensor.1, f32[128,256]{1,0:T(8,128)} %first_in.1, f32[256,256]{1,0:T(8,128)} %second_in.1), custom_call_target="tpu_custom_call" | custom-call | tf_op jit(solution)/shard_map/als/pallas_call | solution.py:593
  86.6 0.8 deliver.1

commit v6 on v5

--- a/solution.py
+++ b/solution.py
@@ -11,7 +11,7 @@
 PASSES = 2
 LANES = 128
 PIVOTS = 16
-GROUP = 4
+GROUP = 8
 CUTS = 2
 MESH = pl.DeviceIdType.MESH
 HIGHEST = lax.Precision.HIGHEST
@@ -161,7 +161,20 @@
 
 def others(axis, n):
     me = lax.axis_index(axis)
-    return [lax.rem(me + d, n) for d in range(1, n)]
+    if n & (n - 1):
+        return [lax.rem(me + d, n) for d in range(1, n)]
+    peers = []
+    for e in range(n - 1, 0, -1):
+        peer = me
+        for bit in (1 << k for k in range(n.bit_length() - 1)):
+            if e & bit:
+                peer = peer + bit - 2 * bit * lax.rem(me // bit, 2)
+        peers.append(peer)
+    return peers
+
+
+def cuts_of(own_second, row):
+    return max(1, min(CUTS, own_second // row // 8))
 
 
 def scatter(axis, n, source, recv, sems, offset=0):
@@ -194,33 +207,6 @@
     for peer in others(axis, n):
         send(parts.at[me, one, :], parts.at[me, one, :], sems, {axis: peer})
     return parts.at[pl.ds(0, n - 1), one, :], sems
-
-
-def scatter_piece(n, cut, source, recv, sems):
-    me = lax.axis_index("row")
-    chunk = recv.shape[1]
-    small = chunk // CUTS
-    inside = pl.ds(cut * small, small)
-
-    def of(peer):
-        return pl.ds(pl.multiple_of(peer * chunk + cut * small, 8), small)
-
-    for peer in others("row", n):
-        send(source.at[of(peer), :], recv.at[me, inside, :], sems.at[cut], {"row": peer})
-    recv[me, cut * small : (cut + 1) * small, :] = source[of(me), :]
-    return recv.at[pl.ds(0, n - 1), inside, :], sems.at[cut]
-
-
-def gather_piece(n, cut, recv, full, sems):
-    me = lax.axis_index("row")
-    chunk = recv.shape[1]
-    small = chunk // CUTS
-    inside = slice(cut * small, (cut + 1) * small)
-    place = pl.ds(pl.multiple_of(me * chunk + cut * small, 8), small)
-    full[place, :] = total(recv[:, inside, :])
-    for peer in others("row", n):
-        send(full.at[place, :], full.at[place, :], sems.at[cut], {"row": peer})
-    return full.at[pl.ds(0, (n - 1) * small), :], sems.at[cut]
 
 
 def lots_out(sums, lots, recv, sems):
@@ -299,6 +285,7 @@
     half = rank // 2
     chips = col // 2
     few = frames // row
+    count = cuts_of(own_second, row)
     buffers = {
         "tens": (frames, own_first, own_second),
         "held": (frames, own_second, rank),
@@ -311,8 +298,9 @@
         "terms_f": (own_first, rank), "recv_f": (col, own_first // col, rank),
         "full_f": (own_first, rank), "parts_w": (row, 8, rank),
     }
-    pairs = ["a", "a2", "a3", "b", "b2", "b3", "f", "f2", "w"]
-    cuts = []
+    pairs = ["a", "a2", "a3", "b", "b2", "b3", "f", "f2", "w"] + list("rdgi")
+    pairs += [name + str(p) for p in range(PASSES) for name in "ch"]
+    cuts = ["s", "t"]
     for p in range(PASSES):
         buffers.update({
             "lots_r%d" % p: (row, few, rank), "recv_r%d" % p: (row, few, rank),
@@ -321,20 +309,18 @@
             "gram_g%d" % p: square, "recv_g%d" % p: (half, rank),
             "across_g%d" % p: (chips, half, rank), "full_g%d" % p: square,
         })
-        pairs += [name + str(p) for name in "rcdghi"]
-        for q in range(rank // LANES):
+        for q in range(count):
             buffers.update({
-                "terms_s%d%d" % (p, q): (own_second, LANES),
-                "recv_s%d%d" % (p, q): (row, own_second // row, LANES),
-                "full_s%d%d" % (p, q): (own_second, LANES),
+                "terms_s%d%d" % (p, q): (own_second // count, rank),
+                "recv_s%d%d" % (p, q): (row, own_second // count // row, rank),
+                "full_s%d%d" % (p, q): (own_second // count, rank),
             })
-            cuts += ["s%d%d" % (p, q), "t%d%d" % (p, q)]
     names = list(buffers) + ["sem_" + name for name in pairs + cuts] + ["sem_load", "sem_move"]
     shapes = [pltpu.VMEM(shape, jnp.float32) for shape in buffers.values()]
     names.insert(len(shapes), "across_left")
     shapes.append(pltpu.VMEM((rank, 6 * PIVOTS), jnp.bfloat16))
     shapes += [pltpu.SemaphoreType.DMA((2,)) for name in pairs]
-    shapes += [pltpu.SemaphoreType.DMA((CUTS, 2)) for name in cuts]
+    shapes += [pltpu.SemaphoreType.DMA((count, 2)) for name in cuts]
     shapes += [pltpu.SemaphoreType.DMA((frames // math.gcd(frames, GROUP),))]
     shapes += [pltpu.SemaphoreType.DMA((2,))]
     return names, shapes
@@ -348,7 +334,7 @@
     frames, own_first, own_second = tensor.shape
     rank = first.shape[1]
     half = rank // 2
-    tiles = rank // LANES
+    count = cuts_of(own_second, row)
     rows_first, rows_second = own_first * row, own_second * col
     steps = rank // PIVOTS
     twin = Twin(col)
@@ -384,16 +370,21 @@
 
         lax.fori_loop(start, stop, step, 0, unroll=4)
 
+    def lines(q):
+        small = own_second // row // count
+        starts = [d * small * count + q * small for d in range(row)]
+        return [slice(start, start + small) for start in starts]
+
     def second_terms(out, q):
-        block = math.gcd(own_second, 128)
-        here = slice(q * LANES, (q + 1) * LANES)
-        for c in range(0, own_second, block):
-            def step(k, total):
-                return total + held[k, c : c + block, here] * frames_out[pl.ds(k, 1), :][:, here]
-
-            out[c : c + block, :] = lax.fori_loop(
-                0, frames, step, jnp.zeros((block, LANES), jnp.float32), unroll=4
-            )
+        small = own_second // row // count
+        zero = tuple(jnp.zeros((small, rank), jnp.float32) for _ in range(row))
+
+        def step(k, totals):
+            weight = frames_out[pl.ds(k, 1), :]
+            return tuple(total + held[k, at, :] * weight for total, at in zip(totals, lines(q)))
+
+        for d, total in enumerate(lax.fori_loop(0, frames, step, zero, unroll=4)):
+            out[d * small : (d + 1) * small, :] = total
 
     def first_terms(raw, start, stop):
         group = math.gcd(stop - start, 4)
@@ -417,15 +408,15 @@
 
     def frames_back(name):
         return lots_share(
-            "row", row, total(v["parts_c" + name]), v["full_r" + name], v["sem_d" + name]
+            "row", row, total(v["parts_c" + name]), v["full_r" + name], v["sem_d"]
         )
 
     def solve_frames(frame_sums, scale):
-        raw = product(frame_sums * scale, inv[...]) * scale
+        raw = product(frame_sums * scale, inv[...], HIGH) * scale
         raw = raw * (1.0 / math.sqrt(rows_first * rows_second))
         normed = raw / jnp.sqrt(jnp.mean(raw * raw, axis=0, keepdims=True) + epsilon)
         frames_out[...] = normed
-        return cross(normed, normed) / frames
+        return cross(normed, normed, HIGH) * (1.0 / frames)
 
     state = (inv, v["panel"], v["solved"], v["across_left"])
 
@@ -454,7 +445,7 @@
     finish(go_b)
     go_b = halves_across(twin, v["gram_b"], v["recv_b"], v["across_b"], v["sem_b2"])
     contract(loads // 2, loads)
-    go_r = lots_out(sums, v["lots_r0"], v["recv_r0"], v["sem_r0"])
+    go_r = lots_out(sums, v["lots_r0"], v["recv_r0"], v["sem_r"])
     finish(go_a)
     go_a = gather("row", row, total(v["recv_a"]), v["full_a"], v["sem_a2"], offset)
     finish(go_b)
@@ -488,41 +479,42 @@
             frame_sums = frame_sums / wide
             frame_scale = first_scale
         frame_gram = solve_frames(frame_sums, frame_scale)
-        parts = [here + str(q) for q in range(tiles)]
-        pieces = [(part, cut) for part in parts for cut in range(CUTS)]
+        parts = [here + str(q) for q in range(count)]
         go_s = []
         for q, part in enumerate(parts):
             second_terms(v["terms_s" + part], q)
-            for cut in range(CUTS):
-                go_s.append(scatter_piece(
-                    row, cut, v["terms_s" + part], v["recv_s" + part], v["sem_s" + part]
-                ))
+            go_s.append(scatter(
+                "row", row, v["terms_s" + part], v["recv_s" + part], v["sem_s"].at[q]
+            ))
         inv[...] = first_gram[...] * frame_gram
         go_t = []
         at = 0
         begin(*state)
-        for q, (part, cut) in enumerate(pieces):
-            until = steps * 7 // 8 if q == 0 else steps
+        for q, part in enumerate(parts):
+            until = steps if q + 1 == count else min(steps, steps * (6 + q) // 8)
             if at < until:
                 invert(*state, at, until)
                 at = until
             finish(go_s[q])
-            go_t.append(gather_piece(
-                row, cut, v["recv_s" + part], v["full_s" + part], v["sem_t" + part]
+            go_t.append(gather(
+                "row", row, total(v["recv_s" + part]), v["full_s" + part], v["sem_t"].at[q]
             ))
         flush(*state)
-        for go in go_t:
-            finish(go)
         raw = v["raw_s" + here]
-        summed = jnp.concatenate([v["full_s" + part][...] for part in parts], axis=1)
-        raw[...] = product(summed * first_scale, inv[...], HIGH) * (
-            first_scale * (1.0 / math.sqrt(rows_first * frames))
-        )
         gram_g, recv_g, across_g, full_g = (
             v[name + here] for name in ("gram_g", "recv_g", "across_g", "full_g")
         )
-        gram_g[...] = cross(raw[...], raw[...], HIGH)
-        go_g = halves_out(twin, gram_g, recv_g, v["sem_g" + here])
+        for q, part in enumerate(parts):
+            finish(go_t[q])
+            some = product(v["full_s" + part][...] * first_scale, inv[...], HIGH) * (
+                first_scale * (1.0 / math.sqrt(rows_first * frames))
+            )
+            small = some.shape[0] // row
+            for d, place in enumerate(lines(q)):
+                raw[place, :] = some[d * small : (d + 1) * small, :]
+            terms = cross(some, some, HIGH)
+            gram_g[...] = terms if q == 0 else gram_g[...] + terms
+        go_g = halves_out(twin, gram_g, recv_g, v["sem_g"])
         last = p + 1 == PASSES
         if last:
             v["terms_f"][...] = jnp.zeros((own_first, rank), jnp.float32)
@@ -530,7 +522,7 @@
         else:
             later = str(p + 1)
             frame_terms(raw, 0, frames)
-            go_r = lots_out(sums, v["lots_r" + later], v["recv_r" + later], v["sem_r" + later])
+            go_r = lots_out(sums, v["lots_r" + later], v["recv_r" + later], v["sem_r"])
         finish(go_g)
         go_g = halves_across(twin, gram_g, recv_g, across_g, v["sem_h" + here])
         if last:
@@ -541,7 +533,7 @@
             go_c = frames_across(later)
         finish(go_g)
         full_g[span(twin.core, half), :] = total(across_g)
-        go_g = halves_back(twin, full_g, v["sem_i" + here])
+        go_g = halves_back(twin, full_g, v["sem_i"])
         finish(go_g)
         gram = full_g[...] * (1.0 / rows_second)
         down = lax.broadcasted_iota(jnp.int32, (rank, rank), 0)
@@ -553,13 +545,13 @@
     inv[...] = second_gram * frame_gram
     second_out[...] = raw[...] / wide
     begin(*state)
-    invert(*state, 0, steps // 2)
+    invert(*state, 0, steps // 8)
     finish(go_f)
     go_f = gather("col", col, total(v["recv_f"]), v["full_f"], v["sem_f2"])
-    invert(*state, steps // 2, steps)
+    invert(*state, steps // 8, steps)
     flush(*state)
     finish(go_f)
-    raw = product(v["full_f"][...] / wide, inv[...]) * (1.0 / math.sqrt(rows_second * frames))
+    raw = product(v["full_f"][...] / wide, inv[...], HIGH) * (1.0 / math.sqrt(rows_second * frames))
     squares = jnp.sum(raw * raw, axis=0, keepdims=True)
     go_w = spread("row", row, squares, v["parts_w"], v["sem_w"])
     first_out[...] = raw

time: 87.6 us -> 83.9 us (0.958)
  Pallas kernels: 86.8 us -> 83.1 us
    pallas_call x1, Pallas kernels: 86 us -> 82.3 us  [body(): pl.pallas_call(functools.partial(kernel, sizes, names), out_shape=shapes,...]
where the time goes in v6:
time: 83.9 us; the launch traced here: 83.8 us
  Pallas kernels  83.1 us (99%)
    pallas_call x1, Pallas kernels, body(): pl.pallas_call(functools.partial(kernel, sizes, names), out_shape=shapes,...  82.3 us

profile of v6, /device:TPU:0, one launch (start us, length us, event | category | flops | bytes accessed | tf_op | source)
XLA Modules:
  0.0 83.8 jit_solution(4017931251937915577)
XLA Ops:
  0.6 82.3 %als.1 = (f32[128,256]{1,0:T(8,128)S(1)}, f32[256,256]{1,0:T(8,128)S(1)}, f32[32,256]{1,0:T(8,128)S(1)}, f32[1,256]{1,0:T(1,128)S(1)}) custom-call(f32[32,128,256]{2,1,0:T(8,128)} %tensor.1, f32[128,256]{1,0:T(8,128)} %first_in.1, f32[256,256]{1,0:T(8,128)} %second_in.1), custom_call_target="tpu_custom_call" | custom-call | tf_op jit(solution)/shard_map/als/pallas_call | solution.py:585
  83.0 0.8 deliver.1

commit v7 on v6

--- a/solution.py
+++ b/solution.py
@@ -12,7 +12,7 @@
 LANES = 128
 PIVOTS = 16
 GROUP = 8
-CUTS = 2
+CUTS = 4
 MESH = pl.DeviceIdType.MESH
 HIGHEST = lax.Precision.HIGHEST
 HIGH = lax.Precision.HIGH
@@ -416,7 +416,6 @@
         raw = raw * (1.0 / math.sqrt(rows_first * rows_second))
         normed = raw / jnp.sqrt(jnp.mean(raw * raw, axis=0, keepdims=True) + epsilon)
         frames_out[...] = normed
-        return cross(normed, normed, HIGH) * (1.0 / frames)
 
     state = (inv, v["panel"], v["solved"], v["across_left"])
 
@@ -478,7 +477,7 @@
         else:
             frame_sums = frame_sums / wide
             frame_scale = first_scale
-        frame_gram = solve_frames(frame_sums, frame_scale)
+        solve_frames(frame_sums, frame_scale)
         parts = [here + str(q) for q in range(count)]
         go_s = []
         for q, part in enumerate(parts):
@@ -486,12 +485,13 @@
             go_s.append(scatter(
                 "row", row, v["terms_s" + part], v["recv_s" + part], v["sem_s"].at[q]
             ))
+        frame_gram = cross(frames_out[...], frames_out[...], HIGH) * (1.0 / frames)
         inv[...] = first_gram[...] * frame_gram
         go_t = []
         at = 0
         begin(*state)
         for q, part in enumerate(parts):
-            until = steps if q + 1 == count else min(steps, steps * (6 + q) // 8)
+            until = steps if q + 1 == count else min(steps, steps * (7 + q) // 8)
             if at < until:
                 invert(*state, at, until)
                 at = until
@@ -543,7 +543,6 @@
         tall = jnp.sqrt(jnp.sum(diagonal, axis=1, keepdims=True) + epsilon)
         second_gram = gram / wide / tall
     inv[...] = second_gram * frame_gram
-    second_out[...] = raw[...] / wide
     begin(*state)
     invert(*state, 0, steps // 8)
     finish(go_f)
@@ -551,10 +550,11 @@
     invert(*state, steps // 8, steps)
     flush(*state)
     finish(go_f)
-    raw = product(v["full_f"][...] / wide, inv[...], HIGH) * (1.0 / math.sqrt(rows_second * frames))
+    second_raw, raw = raw, product(v["full_f"][...] / wide, inv[...], HIGH) * (1.0 / math.sqrt(rows_second * frames))
     squares = jnp.sum(raw * raw, axis=0, keepdims=True)
     go_w = spread("row", row, squares, v["parts_w"], v["sem_w"])
     first_out[...] = raw
+    second_out[...] = second_raw[...] / wide
     finish(go_w)
     weights = jnp.sqrt(total(v["parts_w"])[0:1, :] * (1.0 / rows_first) + epsilon)
     weights_out[...] = weights

time: 83.9 us -> 82.6 us (0.985)
  Pallas kernels: 83.1 us -> 81.8 us
    pallas_call x1, Pallas kernels: 82.3 us -> 81 us  [body(): pl.pallas_call(functools.partial(kernel, sizes, names), out_shape=shapes,...]
where the time goes in v7:
time: 82.6 us; the launch traced here: 82.4 us
  Pallas kernels  81.8 us (99%)
    pallas_call x1, Pallas kernels, body(): pl.pallas_call(functools.partial(kernel, sizes, names), out_shape=shapes,...  81 us

profile of v7, /device:TPU:0, one launch (start us, length us, event | category | flops | bytes accessed | tf_op | source)
XLA Modules:
  0.0 82.4 jit_solution(3169550682232660471)
XLA Ops:
  0.6 81.0 %als.1 = (f32[128,256]{1,0:T(8,128)S(1)}, f32[256,256]{1,0:T(8,128)S(1)}, f32[32,256]{1,0:T(8,128)S(1)}, f32[1,256]{1,0:T(1,128)S(1)}) custom-call(f32[32,128,256]{2,1,0:T(8,128)} %tensor.1, f32[128,256]{1,0:T(8,128)} %first_in.1, f32[256,256]{1,0:T(8,128)} %second_in.1), custom_call_target="tpu_custom_call" | custom-call | tf_op jit(solution)/shard_map/als/pallas_call | solution.py:585
  81.7 0.8 deliver.1

commit v8 on v7

--- a/solution.py
+++ b/solution.py
@@ -11,7 +11,7 @@
 PASSES = 2
 LANES = 128
 PIVOTS = 16
-GROUP = 8
+GROUP = 16
 CUTS = 4
 MESH = pl.DeviceIdType.MESH
 HIGHEST = lax.Precision.HIGHEST

time: 82.6 us -> 82.2 us (level)
  no operation moved by 1% of the time
where the time goes in v8:
time: 82.2 us; the launch traced here: 82 us
  Pallas kernels  81.2 us (99%)
    pallas_call x1, Pallas kernels, body(): pl.pallas_call(functools.partial(kernel, sizes, names), out_shape=shapes,...  80.4 us

profile of v8, /device:TPU:0, one launch (start us, length us, event | category | flops | bytes accessed | tf_op | source)
XLA Modules:
  0.0 82.0 jit_solution(10595540417076642850)
XLA Ops:
  0.6 80.4 %als.1 = (f32[128,256]{1,0:T(8,128)S(1)}, f32[256,256]{1,0:T(8,128)S(1)}, f32[32,256]{1,0:T(8,128)S(1)}, f32[1,256]{1,0:T(1,128)S(1)}) custom-call(f32[32,128,256]{2,1,0:T(8,128)} %tensor.1, f32[128,256]{1,0:T(8,128)} %first_in.1, f32[256,256]{1,0:T(8,128)} %second_in.1), custom_call_target="tpu_custom_call" | custom-call | tf_op jit(solution)/shard_map/als/pallas_call | solution.py:585
  81.1 0.8 deliver.1

commit v9 on v8

--- a/solution.py
+++ b/solution.py
@@ -368,7 +368,7 @@
             sums[pl.ds(k, 1), :] = jnp.sum(held[k] * raw[...], axis=0, keepdims=True)
             return carry
 
-        lax.fori_loop(start, stop, step, 0, unroll=4)
+        lax.fori_loop(start, stop, step, 0, unroll=8)
 
     def lines(q):
         small = own_second // row // count
@@ -383,7 +383,7 @@
             weight = frames_out[pl.ds(k, 1), :]
             return tuple(total + held[k, at, :] * weight for total, at in zip(totals, lines(q)))
 
-        for d, total in enumerate(lax.fori_loop(0, frames, step, zero, unroll=4)):
+        for d, total in enumerate(lax.fori_loop(0, frames, step, zero, unroll=8)):
             out[d * small : (d + 1) * small, :] = total
 
     def first_terms(raw, start, stop):

time: 82.2 us -> 82.2 us (level)
  no operation moved by 1% of the time
where the time goes in v9:
time: 82.2 us; the launch traced here: 82 us
  Pallas kernels  81.2 us (99%)
    pallas_call x1, Pallas kernels, body(): pl.pallas_call(functools.partial(kernel, sizes, names), out_shape=shapes,...  80.4 us

profile of v9, /device:TPU:0, one launch (start us, length us, event | category | flops | bytes accessed | tf_op | source)
XLA Modules:
  0.0 82.0 jit_solution(6219116028848687287)
XLA Ops:
  0.6 80.4 %als.1 = (f32[128,256]{1,0:T(8,128)S(1)}, f32[256,256]{1,0:T(8,128)S(1)}, f32[32,256]{1,0:T(8,128)S(1)}, f32[1,256]{1,0:T(1,128)S(1)}) custom-call(f32[32,128,256]{2,1,0:T(8,128)} %tensor.1, f32[128,256]{1,0:T(8,128)} %first_in.1, f32[256,256]{1,0:T(8,128)} %second_in.1), custom_call_target="tpu_custom_call" | custom-call | tf_op jit(solution)/shard_map/als/pallas_call | solution.py:585
  81.0 0.8 deliver.1
